TPU v7x, 32 devices: a whole 2x2x4 slice. The times are simulated.
32 devices in a mesh: dp: 8 (over y, x, core), seq: 4 (over z).
Axes of the slice: x: 2, y: 2, z: 4, core: 2. Of those that a mesh axis runs over, the one named last changes fastest.
Arguments:
- layer_input: bfloat16 [8, 512, 2048], P('dp', 'seq'), may hold values from -6 to 6
- cotangent: bfloat16 [8, 512, 2048], P('dp', 'seq'), may hold values from -6 to 6
- ln1_gain: float32 [2048], P('dp'), may hold values from 0.5 to 1.5
- ln1_bias: float32 [2048], P('dp'), may hold values from -3 to 3
- w_qkv: bfloat16 [2048, 6144], P('dp'), may hold values from -0.125 to 0.125
- b_qkv: float32 [6144], P('dp'), may hold values from -3 to 3
- w_out: bfloat16 [2048, 2048], P('dp'), may hold values from -0.5 to 0.5
- b_out: float32 [2048], P('dp'), may hold values from -3 to 3
- ln2_gain: float32 [2048], P('dp'), may hold values from 0.5 to 1.5
- ln2_bias: float32 [2048], P('dp'), may hold values from -3 to 3
- w_up: bfloat16 [2048, 8192], P('dp'), may hold values from -0.125 to 0.125
- b_up: float32 [8192], P('dp'), may hold values from -3 to 3
- w_down: bfloat16 [8192, 2048], P('dp'), may hold values from -0.0625 to 0.0625
- b_down: float32 [2048], P('dp'), may hold values from -3 to 3
Outputs:
- output: float32 [8, 512, 2048], P('dp', 'seq')
- input_grad: float32 [8, 512, 2048], P('dp', 'seq')
- ln1_gain_grad: float32 [2048], P('dp')
- ln1_bias_grad: float32 [2048], P('dp')
- w_qkv_grad: float32 [2048, 6144], P('dp')
- b_qkv_grad: float32 [6144], P('dp')
- w_out_grad: float32 [2048, 2048], P('dp')
- b_out_grad: float32 [2048], P('dp')
- ln2_gain_grad: float32 [2048], P('dp')
- ln2_bias_grad: float32 [2048], P('dp')
- w_up_grad: float32 [2048, 8192], P('dp')
- b_up_grad: float32 [8192], P('dp')
- w_down_grad: float32 [8192, 2048], P('dp')
- b_down_grad: float32 [2048], P('dp')
All inputs are finite; a program needn't handle non-finite values.
Results may differ from a plain program's by a relative error of at most 0.029.
Values may be sent and summed in bfloat16 or wider, within the bound.
A program may use at most 640 MiB of HBM per device.

v0:
```python
import jax
import jax.numpy as jnp
from jax import lax
from jax.sharding import PartitionSpec as P

H = 8
HD = 256
ROT = 64


epsilon = 1e-05
masked_fill = -1e30


def normalize(rows, gain, shift):
    center = rows - jnp.mean(rows, axis=-1, keepdims=True)
    factor = lax.rsqrt(jnp.mean(center * center, axis=-1, keepdims=True) + epsilon)
    normed = center * factor
    return (normed, factor, normed * gain + shift)


def normalize_back(incoming, normed, factor, gain):
    scaled = incoming * gain
    return factor * (
        scaled
        - jnp.mean(scaled, axis=-1, keepdims=True)
        - normed * jnp.mean(scaled * normed, axis=-1, keepdims=True)
    )


def gelu_value(inner):
    return inner * 0.5 * (1.0 + jax.scipy.special.erf(inner * 0.7071067811865476))


def gelu_slope(inner):
    cumulative = 0.5 * (1.0 + jax.scipy.special.erf(inner * 0.7071067811865476))
    return cumulative + inner * jnp.exp(-0.5 * inner * inner) * 0.3989422804014327


def angles(positions):
    half = ROT // 2
    freqs = 10000.0 ** (-2.0 * jnp.arange(half).astype(positions.dtype) / ROT)
    theta = positions[:, None] * freqs[None, :]
    return (jnp.cos(theta), jnp.sin(theta))


def rotate(tensor, cosine, sine, direction):
    half = ROT // 2
    first_half = tensor[..., :half]
    second_half = tensor[..., half:ROT]
    return jnp.concatenate(
        [
            first_half * cosine - direction * second_half * sine,
            second_half * cosine + direction * first_half * sine,
            tensor[..., ROT:],
        ],
        axis=-1,
    )


def fetch_forward(gain, shift, matrix, bias, other_matrix, other_bias):
    return (
        lax.all_gather(gain.astype(jnp.bfloat16), "dp", axis=0, tiled=True).astype(gain.dtype),
        lax.all_gather(shift.astype(jnp.bfloat16), "dp", axis=0, tiled=True).astype(shift.dtype),
        lax.all_gather(matrix, "dp", axis=0, tiled=True),
        lax.all_gather(bias.astype(jnp.bfloat16), "dp", axis=0, tiled=True).astype(bias.dtype),
        lax.all_gather(other_matrix, "dp", axis=0, tiled=True),
        lax.all_gather(other_bias.astype(jnp.bfloat16), "dp", axis=0, tiled=True).astype(
            other_bias.dtype
        ),
    )


def fetch_backward(gain, shift, matrix, bias, other_matrix, other_bias):
    return (
        lax.all_gather(gain.astype(jnp.bfloat16), "dp", axis=0, tiled=True).astype(gain.dtype),
        lax.all_gather(shift.astype(jnp.bfloat16), "dp", axis=0, tiled=True).astype(shift.dtype),
        lax.all_gather(matrix, "dp", axis=0, tiled=True),
        lax.all_gather(bias.astype(jnp.bfloat16), "dp", axis=0, tiled=True).astype(bias.dtype),
        lax.all_gather(other_matrix, "dp", axis=0, tiled=True),
        lax.all_gather(other_bias.astype(jnp.bfloat16), "dp", axis=0, tiled=True).astype(
            other_bias.dtype
        ),
    )


def settle(gain_grad, shift_grad, bias_grad, other_bias, left, right, other_left, other_right):
    matrix_grad = jnp.dot(left.T, right, preferred_element_type=jnp.float32)
    other_grad = jnp.dot(other_left.T, other_right, preferred_element_type=jnp.float32)
    shares = (
        lax.psum_scatter(
            gain_grad.astype(jnp.bfloat16), "dp", scatter_dimension=0, tiled=True
        ).astype(jnp.float32),
        lax.psum_scatter(
            shift_grad.astype(jnp.bfloat16), "dp", scatter_dimension=0, tiled=True
        ).astype(jnp.float32),
        lax.psum_scatter(
            matrix_grad.astype(jnp.bfloat16), "dp", scatter_dimension=0, tiled=True
        ).astype(jnp.float32),
        lax.psum_scatter(
            bias_grad.astype(jnp.bfloat16), "dp", scatter_dimension=0, tiled=True
        ).astype(jnp.float32),
        lax.psum_scatter(
            other_grad.astype(jnp.bfloat16), "dp", scatter_dimension=0, tiled=True
        ).astype(jnp.float32),
        lax.psum_scatter(
            other_bias.astype(jnp.bfloat16), "dp", scatter_dimension=0, tiled=True
        ).astype(jnp.float32),
    )
    return (
        lax.psum(shares[0].astype(jnp.bfloat16), "seq").astype(jnp.float32),
        lax.psum(shares[1].astype(jnp.bfloat16), "seq").astype(jnp.float32),
        lax.psum(shares[2].astype(jnp.bfloat16), "seq").astype(jnp.float32),
        lax.psum(shares[3].astype(jnp.bfloat16), "seq").astype(jnp.float32),
        lax.psum(shares[4].astype(jnp.bfloat16), "seq").astype(jnp.float32),
        lax.psum(shares[5].astype(jnp.bfloat16), "seq").astype(jnp.float32),
    )


def block_scores(query_block, key_rows, start):
    scores = jnp.einsum(
        "bqhd,bkhd->bhqk", query_block, key_rows, preferred_element_type=jnp.float32
    ) * HD ** (-0.5)
    length = key_rows.shape[1]
    query_pos = start + jnp.arange(query_block.shape[1], dtype=jnp.int32)
    allowed = jnp.arange(length, dtype=jnp.int32)[None, :] <= query_pos[:, None]
    return jnp.where(allowed[None, None], scores, masked_fill)


def attend(grouped):
    queries = grouped[:, :, 0]
    key_rows = grouped[:, :, 1]
    values = grouped[:, :, 2]
    batch_local, length, local_heads, head_size = queries.shape
    block = min(512, length)
    count = length // block

    def one_block(start):
        query_block = lax.dynamic_slice_in_dim(queries, start, block, 1)
        scores = block_scores(query_block, key_rows, start)
        top = jnp.max(scores, axis=-1, keepdims=True)
        logsum = top[..., 0] + jnp.log(jnp.sum(jnp.exp(scores - top), axis=-1))
        probs = jnp.exp(scores - logsum[..., None]).astype(jnp.bfloat16)
        context = jnp.einsum(
            "bhqk,bkhd->bqhd", probs, values, preferred_element_type=jnp.float32
        ).astype(jnp.bfloat16)
        return (context, logsum)

    starts = jnp.arange(count, dtype=jnp.int32) * block
    contexts, logsums = lax.map(one_block, starts)
    context = jnp.transpose(contexts, (1, 0, 2, 3, 4)).reshape(
        batch_local, length, local_heads, head_size
    )
    logsum = jnp.transpose(logsums, (1, 2, 0, 3)).reshape(batch_local, local_heads, length)
    return (context, logsum)


def attend_back(grouped, context, logsum, incoming):
    queries = grouped[:, :, 0]
    key_rows = grouped[:, :, 1]
    values = grouped[:, :, 2]
    batch_local, length, local_heads, head_size = queries.shape
    block = min(512, length)
    count = length // block
    delta = jnp.sum(incoming.astype(jnp.float32) * context.astype(jnp.float32), axis=-1)

    def one_block(carry, start):
        key_total, value_total = carry
        query_block = lax.dynamic_slice_in_dim(queries, start, block, 1)
        grad_block = lax.dynamic_slice_in_dim(incoming, start, block, 1)
        logsum_block = lax.dynamic_slice_in_dim(logsum, start, block, 2)
        delta_block = jnp.transpose(lax.dynamic_slice_in_dim(delta, start, block, 1), (0, 2, 1))
        scores = block_scores(query_block, key_rows, start)
        probs_f = jnp.exp(scores - logsum_block[..., None])
        probs = probs_f.astype(jnp.bfloat16)
        value_total = value_total + jnp.einsum(
            "bhqk,bqhd->bkhd", probs, grad_block, preferred_element_type=jnp.float32
        )
        prob_grad = jnp.einsum(
            "bqhd,bkhd->bhqk", grad_block, values, preferred_element_type=jnp.float32
        )
        score_grad = (probs_f * (prob_grad - delta_block[..., None]) * HD ** (-0.5)).astype(
            jnp.bfloat16
        )
        query_part = jnp.einsum(
            "bhqk,bkhd->bqhd", score_grad, key_rows, preferred_element_type=jnp.float32
        )
        key_total = key_total + jnp.einsum(
            "bhqk,bqhd->bkhd", score_grad, query_block, preferred_element_type=jnp.float32
        )
        return ((key_total, value_total), query_part)

    empty = jnp.zeros(queries.shape, jnp.float32)
    starts = jnp.arange(count, dtype=jnp.int32) * block
    totals, query_parts = lax.scan(one_block, (empty, empty), starts)
    query_grad = jnp.transpose(query_parts, (1, 0, 2, 3, 4)).reshape(
        batch_local, length, local_heads, head_size
    )
    return jnp.stack([query_grad, totals[0], totals[1]], axis=2).astype(jnp.bfloat16)


def local(
    layer_input,
    cotangent,
    ln1_gain,
    ln1_bias,
    w_qkv,
    b_qkv,
    w_out,
    b_out,
    ln2_gain,
    ln2_bias,
    w_up,
    b_up,
    w_down,
    b_down,
):
    batch_local, tok_local, width = layer_input.shape
    token_count = batch_local * tok_local
    offset = lax.axis_index("seq") * tok_local
    positions = (offset + jnp.arange(tok_local, dtype=jnp.int32)).astype(jnp.float32)
    cosine, sine = angles(positions)
    cosine = cosine[None, :, None, :]
    sine = sine[None, :, None, :]
    gain_one, shift_one, triple_w, triple_b, out_w, out_b = fetch_forward(
        ln1_gain, ln1_bias, w_qkv, b_qkv, w_out, b_out
    )
    rows = layer_input.reshape(token_count, width).astype(jnp.float32)
    normed_one, factor_one, attn_in = normalize(rows, gain_one, shift_one)
    attn_in = attn_in.astype(jnp.bfloat16)
    triple = (jnp.dot(attn_in, triple_w, preferred_element_type=jnp.float32) + triple_b).reshape(
        batch_local, tok_local, 3, H, HD
    )
    queries = rotate(triple[:, :, 0], cosine, sine, 1.0)
    key_rows = rotate(triple[:, :, 1], cosine, sine, 1.0)
    stacked = jnp.stack([queries, key_rows, triple[:, :, 2]], axis=2).astype(jnp.bfloat16)
    grouped = lax.all_to_all(stacked, "seq", split_axis=3, concat_axis=1, tiled=True)
    context, logsum = attend(grouped)
    context_tokens = lax.all_to_all(context, "seq", split_axis=1, concat_axis=2, tiled=True)
    merged = context_tokens.reshape(token_count, width)
    attended = jnp.dot(merged, out_w, preferred_element_type=jnp.float32) + out_b
    gain_two, shift_two, up_w, up_b, down_w, down_b = fetch_forward(
        ln2_gain, ln2_bias, w_up, b_up, w_down, b_down
    )
    normed_two, factor_two, mlp_in = normalize(rows, gain_two, shift_two)
    mlp_in = mlp_in.astype(jnp.bfloat16)
    inner = jnp.dot(mlp_in, up_w, preferred_element_type=jnp.float32) + up_b
    hidden = gelu_value(inner).astype(jnp.bfloat16)
    output = rows + attended + jnp.dot(hidden, down_w, preferred_element_type=jnp.float32) + down_b
    incoming = cotangent.reshape(token_count, width)
    grad_rows = incoming.astype(jnp.float32)
    gain_two, shift_two, up_w, up_b, down_w, down_b = fetch_backward(
        ln2_gain, ln2_bias, w_up, b_up, w_down, b_down
    )
    b_down_grad = jnp.sum(grad_rows, axis=0)
    inner_grad = jnp.dot(incoming, down_w.T, preferred_element_type=jnp.float32) * gelu_slope(inner)
    inner_grad_b = inner_grad.astype(jnp.bfloat16)
    b_up_grad = jnp.sum(inner_grad, axis=0)
    mlp_in_grad = jnp.dot(inner_grad_b, up_w.T, preferred_element_type=jnp.float32)
    ln2_gain_grad = jnp.sum(mlp_in_grad * normed_two, axis=0)
    ln2_bias_grad = jnp.sum(mlp_in_grad, axis=0)
    mlp_grads = settle(
        ln2_gain_grad, ln2_bias_grad, b_up_grad, b_down_grad, mlp_in, inner_grad_b, hidden, incoming
    )
    mlp_back = normalize_back(mlp_in_grad, normed_two, factor_two, gain_two)
    gain_one, shift_one, triple_w, triple_b, out_w, out_b = fetch_backward(
        ln1_gain, ln1_bias, w_qkv, b_qkv, w_out, b_out
    )
    b_out_grad = jnp.sum(grad_rows, axis=0)
    context_grad = (
        jnp.dot(incoming, out_w.T, preferred_element_type=jnp.float32)
        .astype(jnp.bfloat16)
        .reshape(batch_local, tok_local, H, HD)
    )
    grouped_grad = lax.all_to_all(context_grad, "seq", split_axis=2, concat_axis=1, tiled=True)
    triple_heads = attend_back(grouped, context, logsum, grouped_grad)
    token_grad = lax.all_to_all(
        triple_heads, "seq", split_axis=1, concat_axis=3, tiled=True
    ).astype(jnp.float32)
    query_back = rotate(token_grad[:, :, 0], cosine, sine, -1.0)
    key_back = rotate(token_grad[:, :, 1], cosine, sine, -1.0)
    triple_grad = jnp.stack([query_back, key_back, token_grad[:, :, 2]], axis=2).reshape(
        token_count, 3 * width
    )
    triple_grad_b = triple_grad.astype(jnp.bfloat16)
    b_qkv_grad = jnp.sum(triple_grad, axis=0)
    attn_in_grad = jnp.dot(triple_grad_b, triple_w.T, preferred_element_type=jnp.float32)
    ln1_gain_grad = jnp.sum(attn_in_grad * normed_one, axis=0)
    ln1_bias_grad = jnp.sum(attn_in_grad, axis=0)
    attn_grads = settle(
        ln1_gain_grad,
        ln1_bias_grad,
        b_qkv_grad,
        b_out_grad,
        attn_in,
        triple_grad_b,
        merged,
        incoming,
    )
    grad_total = (
        grad_rows + normalize_back(attn_in_grad, normed_one, factor_one, gain_one) + mlp_back
    )
    return (
        output.reshape(layer_input.shape),
        grad_total.reshape(layer_input.shape),
        attn_grads[0],
        attn_grads[1],
        attn_grads[2],
        attn_grads[3],
        attn_grads[4],
        attn_grads[5],
        mlp_grads[0],
        mlp_grads[1],
        mlp_grads[2],
        mlp_grads[3],
        mlp_grads[4],
        mlp_grads[5],
    )


def solution(mesh):
    in_specs = (
        P("dp", "seq", None),
        P("dp", "seq", None),
        P("dp"),
        P("dp"),
        P("dp", None),
        P("dp"),
        P("dp", None),
        P("dp"),
        P("dp"),
        P("dp"),
        P("dp", None),
        P("dp"),
        P("dp", None),
        P("dp"),
    )
    out_specs = (
        P("dp", "seq", None),
        P("dp", "seq", None),
        P("dp"),
        P("dp"),
        P("dp", None),
        P("dp"),
        P("dp", None),
        P("dp"),
        P("dp"),
        P("dp"),
        P("dp", None),
        P("dp"),
        P("dp", None),
        P("dp"),
    )
    return jax.shard_map(local, mesh=mesh, in_specs=in_specs, out_specs=out_specs, check_vma=False)
```

profile of v0, /device:TPU:0, one launch (start us, length us, event | category | flops | bytes accessed | tf_op | source)
XLA Modules:
  0.0 1625.4 jit_solution(7226123091825915187)
XLA Ops:
  10.1 10.6 all-gather.2
  20.7 9.2 all-gather.1
  30.0 8.1 all-gather
  38.8 28.2 %all-gather.14.cloned.1.call-done = bf16[2048,2048]{1,0:T(8,128)(2,1)} async-done(((bf16[256,2048]{1,0:T(8,128)(2,1)}), bf16[2048,2048]{1,0:T(8,128)(2,1)}) %all-gather.14.cloned.1.call-update) | async-done | bytes 8388624 | tf_op jit(solution)/shard_map/all_gather | solution.py:67
  66.9 6.3 convolution_convert_fusion.4
  78.8 115.2 %all-gather.12.cloned.1.call-done = bf16[2048,6144]{1,0:T(8,128)(2,1)} async-done(((bf16[256,6144]{1,0:T(8,128)(2,1)}), bf16[2048,6144]{1,0:T(8,128)(2,1)}) %all-gather.12.cloned.1.call-update) | async-done | bytes 25165840 | tf_op jit(solution)/shard_map/all_gather | solution.py:65
  194.0 13.4 convolution_add_fusion.1
  226.8 32.4 %all-to-all-done = bf16[1,128,3,8,256]{1,4,2,0,3:T(8,128)(2,1)S(1)} async-done(((bf16[1,128,3,8,256]{1,4,2,0,3:T(8,128)(2,1)}), bf16[1,128,3,8,256]{1,4,2,0,3:T(8,128)(2,1)S(1)}, u32[]{:S(2)}, u32[]{:S(2)}) %all-to-all-start) | async-done | bytes 1572896 | tf_op jit(solution)/shard_map/all_to_all | solution.py:237
  265.8 16.6 %all_to_all.57 = bf16[1,512,2,256]{3,2,0,1:T(2,128)(2,1)S(1)} all-to-all(bf16[1,512,2,256]{3,2,0,1:T(2,128)(2,1)S(1)} %copy.88), channel_id=1, replica_groups=mesh['dp'=8,'seq'=4] {'seq'}, dimensions={1} | all-to-all | bytes 1048576 | tf_op jit(solution)/shard_map/all_to_all | solution.py:239
  297.6 39.6 %all_to_all.58 = bf16[1,512,3,2,256]{4,3,2,0,1:T(2,128)(2,1)S(1)} all-to-all(bf16[1,512,3,2,256]{4,3,2,0,1:T(2,128)(2,1)} %copy.101), channel_id=1, replica_groups=mesh['dp'=8,'seq'=4] {'seq'}, dimensions={1} | all-to-all | bytes 3145728 | tf_op jit(solution)/shard_map/all_to_all | solution.py:277
  344.4 12.4 convolution_convert_fusion.2
  357.5 8.9 all_gather.51
  366.4 8.1 all-gather.5
  374.5 9.4 all-gather.4
  384.0 17.2 %convolution_add_fusion = f32[128,8192]{1,0:T(8,128)} fusion(bf16[2048,8192]{1,0:T(8,128)(2,1)} %all-gather.16.cloned.1.call-done, f32[8192]{0:T(1024)S(1)} %convert_element_type.309, bf16[1,128,2048]{2,1,0:T(8,128)(2,1)S(1)} %copy-done.1, f32[2048]{0:T(1024)S(1)} %bitcast.228, f32[2048]{0:T(1024)S(1)} %bitcast.222, f32[128]{0:T(128)S(1)} %add_rsqrt_fusion, ...), kind=kOutput, calls=%fused_computation.4 | convolution fusion | flops 4297588736 | bytes 38323200 | tf_op jit(solution)/shard_map/dot_general | solution.py:247
  401.2 117.9 %all-gather.18.cloned.1.call-done = bf16[8192,2048]{1,0:T(8,128)(2,1)} async-done(((bf16[1024,2048]{1,0:T(8,128)(2,1)}), bf16[8192,2048]{1,0:T(8,128)(2,1)}) %all-gather.18.cloned.1.call-update) | async-done | bytes 33554448 | tf_op jit(solution)/shard_map/all_gather | solution.py:67
  519.1 19.8 %fusion.68 = (bf16[8192]{0:T(1024)(128)(2,1)S(1)}, bf16[128,8192]{1,0:T(8,128)(2,1)}) fusion(f32[128,8192]{1,0:T(8,128)} %convolution_add_fusion, bf16[8192,2048]{1,0:T(8,128)(2,1)} %all-gather.18.cloned.1.call-done, bf16[1,128,2048]{2,1,0:T(8,128)(2,1)S(1)} %copy-done.4), kind=kOutput, calls=%fused_computation.128 | convolution fusion | flops 4306493440 | bytes 40386560 | tf_op jit(solution)/shard_map/dot_general | solution.py:256
  538.9 16.0 convolution_convert_fusion
  555.1 16.3 %convolution_convert_fusion.1 = bf16[8192,2048]{1,0:T(8,128)(2,1)} fusion(bf16[1,128,2048]{2,1,0:T(8,128)(2,1)S(1)} %copy-done.4, f32[128,8192]{1,0:T(8,128)} %convolution_add_fusion), kind=kOutput, calls=%fused_computation.1 | convolution fusion | flops 4316987392 | bytes 38273024 | tf_op jit(solution)/shard_map/dot_general | solution.py:89
  571.5 23.0 %reduce-scatter.7.cloned.1.call-done = bf16[256,2048]{1,0:T(8,128)(2,1)} async-done(((bf16[2048,2048]{1,0:T(8,128)(2,1)}), bf16[256,2048]{1,0:T(8,128)(2,1)}) %reduce-scatter.7.cloned.1.call-update) | async-done | bytes 1048592 | tf_op jit(solution)/shard_map/reduce_scatter | solution.py:103
  594.5 159.8 %reduce-scatter.5.cloned.1.call-done = bf16[256,6144]{1,0:T(8,128)(2,1)} async-done(((bf16[2048,6144]{1,0:T(8,128)(2,1)}), bf16[256,6144]{1,0:T(8,128)(2,1)}) %reduce-scatter.5.cloned.1.call-update) | async-done | bytes 3145744 | tf_op jit(solution)/shard_map/reduce_scatter | solution.py:97
  754.3 209.1 %reduce-scatter.9.cloned.1.call-done = bf16[256,8192]{1,0:T(8,128)(2,1)} async-done(((bf16[2048,8192]{1,0:T(8,128)(2,1)}), bf16[256,8192]{1,0:T(8,128)(2,1)}) %reduce-scatter.9.cloned.1.call-update) | async-done | bytes 4194320 | tf_op jit(solution)/shard_map/reduce_scatter | solution.py:97
  963.4 209.1 %reduce-scatter.11.cloned.1.call-done = bf16[1024,2048]{1,0:T(8,128)(2,1)} async-done(((bf16[8192,2048]{1,0:T(8,128)(2,1)}), bf16[1024,2048]{1,0:T(8,128)(2,1)}) %reduce-scatter.11.cloned.1.call-update) | async-done | bytes 4194320 | tf_op jit(solution)/shard_map/reduce_scatter | solution.py:103
  1173.1 8.9 all-gather.3
  1182.0 8.0 all-gather.6
  1192.7 6.1 fusion.6
  1200.4 17.1 %fusion.46 = f32[128,2048]{1,0:T(8,128)} fusion(bf16[2048,8192]{1,0:T(8,128)(2,1)} %all-gather.16.cloned.1.call-done, bf16[128,8192]{1,0:T(8,128)(2,1)S(1)} %copy-done.5), kind=kOutput, calls=%fused_computation.80 | convolution fusion | flops 4294967296 | bytes 36700160 | tf_op jit(solution)/shard_map/dot_general | solution.py:259
  1217.5 14.5 fusion.38
  1232.0 25.7 %all-reduce.7 = (bf16[2048]{0:T(1024)(128)(2,1)S(1)}, bf16[2048]{0:T(1024)(128)(2,1)S(1)}, bf16[6144]{0:T(1024)(128)(2,1)S(1)}, bf16[2048]{0:T(1024)(128)(2,1)S(...) all-reduce(bf16[2048]{0:T(1024)(128)(2,1)S(1)} %get-tuple-element.6, ...), channel_id=2, replica_groups=mesh['dp'=8,'seq'=4] {'dp'}, use_global_device_ids=true, to_apply=%region_10.11.clone | all-reduce | flops 24576 | bytes 98304
  1258.1 14.3 all-reduce.8
  1279.3 14.6 fusion.5
  1293.9 308.1 %all-reduce.12.cloned.1.call-done = (bf16[256,6144]{1,0:T(8,128)(2,1)}, bf16[256,2048]{1,0:T(8,128)(2,1)}, bf16[256,8192]{1,0:T(8,128)(2,1)}, bf16[1024,2048]{1,0:T(8,128)(2,1)}) async-done(((bf16[256,6144]{1,0:T(8,128)(2,1)}, bf16[256,2048]{1,0:T(8,128)(2,1)}, bf16[256,8192]{1,0:T(8,128)(2,1)}, bf16[1024,2048]{1,0:T(8,128)(2,1)}), (bf16[256,6144]{1,0:T(8,128)(2,1)}, bf16[256,2048]{1,0:T(8,128)(2,1)}, ...) | async-done | bytes 12582928 | tf_op jit(solution)/shard_map/psum | solution.py:113
  (176 shorter events, 85.0 us)
Async XLA Ops:
  7.2 59.8 %all-gather.14.cloned.1.call-start = ((), (), s32[]{:S(2)}) async-start(), calls=%async_computation.9 | async-start | bytes 9437184 | tf_op jit(solution)/shard_map/all_gather | solution.py:67
  7.9 186.1 %all-gather.12.cloned.1.call-start = ((), (), s32[]{:S(2)}) async-start(), calls=%async_computation.8 | async-start | bytes 28311552 | tf_op jit(solution)/shard_map/all_gather | solution.py:65
  8.7 375.3 %all-gather.16.cloned.1.call-start = ((), (), s32[]{:S(2)}) async-start(), calls=%async_computation.10 | async-start | bytes 37748736 | tf_op jit(solution)/shard_map/all_gather | solution.py:65
  9.4 11.3 copy-start.22
  9.4 20.5 %copy-start.23 = (f32[256]{0:T(256)S(1)}, f32[256]{0:T(256)}, u32[]{:S(2)}) copy-start(f32[256]{0:T(256)} %param.16) | copy-start | bytes 3076
  9.4 28.7 %copy-start.1 = (bf16[1,128,2048]{2,1,0:T(8,128)(2,1)S(1)}, bf16[1,128,2048]{2,1,0:T(8,128)(2,1)}, u32[]{:S(2)}) copy-start(bf16[1,128,2048]{2,1,0:T(8,128)(2,1)} %param.14) | copy-start | bytes 1572868
  9.4 57.5 %copy-start.4 = (bf16[1,128,2048]{2,1,0:T(8,128)(2,1)S(1)}, bf16[1,128,2048]{2,1,0:T(8,128)(2,1)}, u32[]{:S(2)}) copy-start(bf16[1,128,2048]{2,1,0:T(8,128)(2,1)} %param.15) | copy-start | bytes 1572868
  9.4 509.6 %all-gather.18.cloned.1.call-start = ((), (), s32[]{:S(2)}) async-start(), calls=%async_computation.11 | async-start | bytes 37748736 | tf_op jit(solution)/shard_map/all_gather | solution.py:67
  74.2 142.1 %all-to-all-start.2 = ((bf16[1,128,8,256]{3,1,0,2:T(8,128)(2,1)}), bf16[1,128,8,256]{3,1,0,2:T(8,128)(2,1)S(1)}, u32[]{:S(2)}, u32[]{:S(2)}) async-start(bf16[1,128,8,256]{3,1,0,2:T(8,128)(2,1)} %copy.91), calls=%async_computation.2 | async-start | bytes 1048576 | tf_op jit(solution)/shard_map/all_to_all | solution.py:275
  217.1 42.1 %all-to-all-start = ((bf16[1,128,3,8,256]{1,4,2,0,3:T(8,128)(2,1)}), bf16[1,128,3,8,256]{1,4,2,0,3:T(8,128)(2,1)S(1)}, u32[]{:S(2)}, u32[]{:S(2)}) async-start(bf16[1,128,3,8,256]{1,4,2,0,3:T(8,128)(2,1)} %copy.84), calls=%async_computation | async-start | bytes 3145728 | tf_op jit(solution)/shard_map/all_to_all | solution.py:237
  221.9 372.6 %reduce-scatter.7.cloned.1.call-start = ((), (), s32[]{:S(2)}) async-start(), calls=%async_computation.13 | async-start | bytes 9437184 | tf_op jit(solution)/shard_map/reduce_scatter | solution.py:103
  260.8 2.5 copy-start.17
  263.0 2.4 copy-start.2
  282.8 5.7 copy-start.6
  288.5 465.7 %reduce-scatter.5.cloned.1.call-start = ((), (), s32[]{:S(2)}) async-start(), calls=%async_computation.12 | async-start | bytes 28311552 | tf_op jit(solution)/shard_map/reduce_scatter | solution.py:97
  292.3 1.6 copy-start.3
  356.8 9.6 copy-start.24
  356.8 17.7 %copy-start.25 = (f32[256]{0:T(256)S(1)}, f32[256]{0:T(256)}, u32[]{:S(2)}) copy-start(f32[256]{0:T(256)} %param.22) | copy-start | bytes 3076
  356.8 606.5 %reduce-scatter.9.cloned.1.call-start = ((), (), s32[]{:S(2)}) async-start(), calls=%async_computation.14 | async-start | bytes 37748736 | tf_op jit(solution)/shard_map/reduce_scatter | solution.py:97
  554.9 617.5 %reduce-scatter.11.cloned.1.call-start = ((), (), s32[]{:S(2)}) async-start(), calls=%async_computation.15 | async-start | bytes 37748736 | tf_op jit(solution)/shard_map/reduce_scatter | solution.py:103
  571.4 1030.6 %all-reduce.12.cloned.1.call-start = ((), (), s32[]{:S(2)}) async-start(), calls=%async_computation.16 | async-start | bytes 25165824 | tf_op jit(solution)/shard_map/psum | solution.py:113
  1172.4 9.6 copy-start.27
  1172.4 17.7 %copy-start.28 = (u32[32]{0:T(128)S(1)}, u32[32]{0:T(128)}, u32[]{:S(2)}) copy-start(u32[32]{0:T(128)} %constant.88) | copy-start | bytes 388
  1192.7 6.1 copy-start.8
  1192.7 6.1 copy-start.10
  1192.7 6.1 copy-start.12
  1198.8 1.6 copy-start.5
  1272.5 6.8 copy-start
  1274.2 343.7 %copy-start.21 = (f32[256]{0:T(256)}, f32[256]{0:T(256)S(1)}, u32[]{:S(2)}) copy-start(f32[256]{0:T(256)S(1)} %convert_element_type.339) | copy-start | bytes 3076
  1602.0 5.5 copy-start.18
  1602.0 7.1 copy-start.16
  1609.1 4.4 copy-start.15
  (8 other events, 8.1 us)
Sparse Core Ops, SparseCore 0:
  9.9 57.0 all-gather.13
  68.8 125.1 all-gather.11
  195.9 160.6 all-gather.15
  358.4 160.6 all-gather.17
  523.0 71.4 reduce-scatter.6
  598.0 156.2 reduce-scatter.4
  757.8 205.4 reduce-scatter.8
  966.9 205.4 reduce-scatter.10
  1175.3 426.6 all-reduce.11
where the time goes:
time: 1630 us
  waiting for transfers between devices  1210 us (74%)
  blocking collectives  167 us (10%)
  matrix products  167 us (10%)
  local copies, waits for them, and re-layouts  32.8 us (2%)
  other arithmetic  25.8 us (2%)
  between operations  16.8 us (1%)
    reduce_scatter x2, waiting for transfers between devices, settle(): lax.psum_scatter(matrix_grad.astype(jnp.bfloat16), 'dp', scatter_dimensio...  369 us
    psum x1, waiting for transfers between devices, settle(): lax.psum(shares[2].astype(jnp.bfloat16), 'seq').astype(jnp.float32)  308 us
    reduce_scatter x2, waiting for transfers between devices, settle(): lax.psum_scatter(other_grad.astype(jnp.bfloat16), 'dp', scatter_dimension...  232 us
    all_gather x2, waiting for transfers between devices, fetch_forward(): lax.all_gather(other_matrix, 'dp', axis=0, tiled=True)  146 us
    all_gather x2, waiting for transfers between devices, fetch_forward(): lax.all_gather(matrix, 'dp', axis=0, tiled=True)  115 us
    all_to_all x1, blocking collectives, local(): lax.all_to_all(triple_heads, 'seq', split_axis=1, concat_axis=3, tiled=True)  39.6 us
  transfers between devices with their start and end apart: 11, of which 9 were waited for; matrix products, arithmetic and copies ran while one was open for 13% of the time, Pallas kernels for 0%

commit v1 on v0

v1 whole, which is shorter than its diff:
```python
import jax
import jax.numpy as jnp
from jax import lax
from jax.sharding import PartitionSpec as P

H = 8
HD = 256
ROT = 64

epsilon = 1e-05
masked_fill = -1e30


def dot(a, b, contract):
    return lax.dot_general(a, b, (contract, ((), ())), preferred_element_type=jnp.float32)


def normalize(rows):
    center = rows - jnp.mean(rows, axis=-1, keepdims=True)
    factor = lax.rsqrt(jnp.mean(center * center, axis=-1, keepdims=True) + epsilon)
    return center * factor, factor


def angles(positions):
    half = ROT // 2
    freqs = 10000.0 ** (-2.0 * jnp.arange(half).astype(positions.dtype) / ROT)
    theta = positions[:, None] * freqs[None, :]
    return (jnp.cos(theta), jnp.sin(theta))


def rotate(tensor, cosine, sine, direction):
    half = ROT // 2
    first_half = tensor[..., :half]
    second_half = tensor[..., half:ROT]
    return jnp.concatenate(
        [
            first_half * cosine - direction * second_half * sine,
            second_half * cosine + direction * first_half * sine,
            tensor[..., ROT:],
        ],
        axis=-1,
    )


def gather_dp(rows):
    return lax.all_gather(rows, "dp", axis=0, tiled=True)


def gather_seq(shard):
    return lax.all_gather(shard, "seq", axis=0, tiled=False)


def scatter_dp(rows):
    return lax.psum_scatter(rows, "dp", scatter_dimension=0, tiled=True)


def exchange_sum(partial, n_seq):
    slabs = partial.astype(jnp.bfloat16).reshape(n_seq, partial.shape[0] // n_seq, partial.shape[1])
    got = lax.all_to_all(slabs, "seq", split_axis=0, concat_axis=0, tiled=True)
    return jnp.sum(got.astype(jnp.float32), axis=0)


def make_local(n_dp, n_seq):
    def local(
        layer_input,
        cotangent,
        ln1_gain,
        ln1_bias,
        w_qkv,
        b_qkv,
        w_out,
        b_out,
        ln2_gain,
        ln2_bias,
        w_up,
        b_up,
        w_down,
        b_down,
    ):
        f32, bf16 = jnp.float32, jnp.bfloat16
        _, tok_local, width = layer_input.shape
        length = tok_local * n_seq
        own = width // n_dp
        ff = w_up.shape[1]
        ff_own = ff // n_dp
        unit = ff_own // n_seq
        heads = H // n_seq
        z = lax.axis_index("seq")

        up_own = lax.dynamic_index_in_dim(
            w_up.reshape(own, n_dp, n_seq, unit), z, 2, keepdims=False
        ).reshape(own, n_dp * unit)
        up_w = gather_dp(up_own)
        down_own = lax.dynamic_slice_in_dim(w_down, z * unit, unit, 0)
        down_w = gather_dp(down_own)
        qkv_own = lax.dynamic_slice_in_dim(
            w_qkv.reshape(own, 3, H, HD), z * heads, heads, 2
        ).reshape(own, 3 * heads * HD)
        triple_w = gather_dp(qkv_own)
        owners = n_dp // n_seq
        piece = own // n_dp
        spread = lax.all_to_all(
            w_out.reshape(n_dp, piece, width), "dp", split_axis=0, concat_axis=0, tiled=True
        )
        out_own = lax.dynamic_slice_in_dim(spread, z * owners, owners, 0)
        out_w = (
            lax.all_gather(out_own, "dp", axis=0, tiled=False)
            .transpose(1, 0, 2, 3)
            .reshape(owners * own, width)
        )

        packed = jnp.concatenate(
            [ln1_gain, ln1_bias, ln2_gain, ln2_bias, b_out, b_down, b_qkv, b_up]
        )
        gathered = lax.all_gather(packed, "dp", axis=0, tiled=False)
        gain_one, shift_one, gain_two, shift_two, out_b, down_b = (
            gathered[:, k * own : (k + 1) * own].reshape(width) for k in range(6)
        )
        base = 6 * own
        triple_b = lax.dynamic_slice_in_dim(
            gathered[:, base : base + 3 * own].reshape(3, H, HD), z * heads, heads, 1
        ).reshape(3 * heads * HD)
        up_b = lax.dynamic_index_in_dim(
            gathered[:, base + 3 * own :].reshape(n_dp, n_seq, unit), z, 1, keepdims=False
        ).reshape(n_dp * unit)

        tokens = gather_seq(layer_input.reshape(tok_local, width)).reshape(length, width)
        incoming = gather_seq(cotangent.reshape(tok_local, width)).reshape(length, width)

        normed, _ = normalize(tokens.astype(f32))
        mlp_in = (normed * gain_two + shift_two).astype(bf16)
        attn_in = (normed * gain_one + shift_one).astype(bf16)

        inner = dot(mlp_in, up_w, ((1,), (0,))) + up_b
        cumulative = 0.5 * (1.0 + lax.erf(inner * 0.7071067811865476))
        hidden = (inner * cumulative).astype(bf16)
        slope = cumulative + inner * jnp.exp(-0.5 * inner * inner) * 0.3989422804014327
        down_grad = dot(hidden, incoming, ((0,), (0,))).astype(bf16)
        inner_grad = dot(incoming, down_w, ((1,), (1,))) * slope
        inner_grad_b = inner_grad.astype(bf16)
        up_grad = dot(mlp_in, inner_grad_b, ((0,), (0,))).astype(bf16)
        mlp_out = dot(hidden, down_w, ((1,), (0,)))
        mlp_in_grad = dot(inner_grad_b, up_w, ((1,), (1,)))
        b_up_grad = jnp.sum(inner_grad, axis=0)
        ln2_gain_grad = jnp.sum(mlp_in_grad * normed, axis=0)
        ln2_bias_grad = jnp.sum(mlp_in_grad, axis=0)

        cosine, sine = angles(jnp.arange(length, dtype=jnp.int32).astype(f32))
        cosine, sine = cosine[:, None, :], sine[:, None, :]
        triple = (dot(attn_in, triple_w, ((1,), (0,))) + triple_b).reshape(length, 3, heads, HD)
        queries = rotate(triple[:, 0], cosine, sine, 1.0).astype(bf16)
        key_rows = rotate(triple[:, 1], cosine, sine, 1.0).astype(bf16)
        values = triple[:, 2].astype(bf16)
        scores = jnp.einsum("qhd,khd->hqk", queries, key_rows, preferred_element_type=f32) * HD ** (
            -0.5
        )
        order = jnp.arange(length, dtype=jnp.int32)
        scores = jnp.where((order[None, :] <= order[:, None])[None], scores, masked_fill)
        top = jnp.max(scores, axis=-1, keepdims=True)
        logsum = top + jnp.log(jnp.sum(jnp.exp(scores - top), axis=-1, keepdims=True))
        probs_f = jnp.exp(scores - logsum)
        probs = probs_f.astype(bf16)
        context = jnp.einsum("hqk,khd->qhd", probs, values, preferred_element_type=f32).astype(bf16)
        merged = context.reshape(length, heads * HD)
        attended = dot(merged, out_w, ((1,), (0,)))
        out_grad = dot(merged, incoming, ((0,), (0,))).astype(bf16)
        context_grad = dot(incoming, out_w, ((1,), (1,))).astype(bf16).reshape(length, heads, HD)
        delta = jnp.sum(context_grad.astype(f32) * context.astype(f32), axis=-1)
        value_grad = jnp.einsum(
            "hqk,qhd->khd", probs, context_grad, preferred_element_type=f32
        ).astype(bf16)
        prob_grad = jnp.einsum("qhd,khd->hqk", context_grad, values, preferred_element_type=f32)
        score_grad = (probs_f * (prob_grad - delta.T[:, :, None]) * HD ** (-0.5)).astype(bf16)
        query_grad = jnp.einsum(
            "hqk,khd->qhd", score_grad, key_rows, preferred_element_type=f32
        ).astype(bf16)
        key_grad = jnp.einsum(
            "hqk,qhd->khd", score_grad, queries, preferred_element_type=f32
        ).astype(bf16)
        triple_grad = jnp.stack(
            [
                rotate(query_grad.astype(f32), cosine, sine, -1.0),
                rotate(key_grad.astype(f32), cosine, sine, -1.0),
                value_grad.astype(f32),
            ],
            axis=1,
        ).reshape(length, 3 * heads * HD)
        triple_grad_b = triple_grad.astype(bf16)
        b_qkv_grad = jnp.sum(triple_grad, axis=0)
        qkv_grad = dot(attn_in, triple_grad_b, ((0,), (0,))).astype(bf16)
        attn_in_grad = dot(triple_grad_b, triple_w, ((1,), (1,)))
        ln1_gain_grad = jnp.sum(attn_in_grad * normed, axis=0)
        ln1_bias_grad = jnp.sum(attn_in_grad, axis=0)

        rows = layer_input.reshape(tok_local, width).astype(f32)
        grad_rows = cotangent.reshape(tok_local, width).astype(f32)
        output = rows + (out_b + down_b) + exchange_sum(attended + mlp_out, n_seq)
        scaled = exchange_sum(attn_in_grad * gain_one + mlp_in_grad * gain_two, n_seq)
        normed_own, factor_own = normalize(rows)
        input_grad = grad_rows + factor_own * (
            scaled
            - jnp.mean(scaled, axis=-1, keepdims=True)
            - normed_own * jnp.mean(scaled * normed_own, axis=-1, keepdims=True)
        )

        down_part = gather_seq(scatter_dp(down_grad))
        down_full = down_part.reshape(ff_own, width).astype(f32)
        up_part = gather_seq(scatter_dp(up_grad))
        up_full = (
            up_part.reshape(n_seq, own, n_dp, unit).transpose(1, 2, 0, 3).reshape(own, ff)
        ).astype(f32)
        out_part = gather_seq(
            scatter_dp(
                out_grad.reshape(owners, n_dp, piece, width)
                .transpose(1, 0, 2, 3)
                .reshape(n_dp * owners * piece, width)
            )
        )
        out_full = (
            lax.all_to_all(
                out_part.reshape(n_dp, piece, width), "dp", split_axis=0, concat_axis=0, tiled=True
            )
            .reshape(own, width)
            .astype(f32)
        )
        qkv_part = gather_seq(scatter_dp(qkv_grad))
        qkv_full = (
            qkv_part.reshape(n_seq, own, 3, heads * HD)
            .transpose(1, 2, 0, 3)
            .reshape(own, 3 * width)
            .astype(f32)
        )

        here = jnp.arange(n_seq) == z
        b_up_wide = jnp.where(
            here[None, :, None], b_up_grad.reshape(n_dp, 1, unit), 0.0
        ).reshape(n_dp, ff_own)
        b_qkv_wide = jnp.where(
            here[None, :, None], b_qkv_grad.reshape(3, 1, heads * HD), 0.0
        ).reshape(n_dp, 3 * own)
        b_down_grad = jnp.sum(grad_rows, axis=0)
        small = jnp.concatenate(
            [
                ln1_gain_grad.reshape(n_dp, own),
                ln1_bias_grad.reshape(n_dp, own),
                ln2_gain_grad.reshape(n_dp, own),
                ln2_bias_grad.reshape(n_dp, own),
                b_down_grad.reshape(n_dp, own),
                b_qkv_wide,
                b_up_wide,
            ],
            axis=1,
        )
        small = lax.psum(small, ("dp", "seq"))
        mine = lax.dynamic_index_in_dim(small, lax.axis_index("dp"), 0, keepdims=False)
        g1, s1, g2, s2, bd = (mine[k * own : (k + 1) * own] for k in range(5))
        bq = mine[5 * own : 8 * own]
        bu = mine[8 * own :]

        return (
            output.reshape(layer_input.shape),
            input_grad.reshape(layer_input.shape),
            g1,
            s1,
            qkv_full,
            bq,
            out_full,
            bd,
            g2,
            s2,
            up_full,
            bu,
            down_full,
            bd,
        )

    return local


def solution(mesh):
    vector, matrix, tokens = P("dp"), P("dp", None), P("dp", "seq", None)
    in_specs = (
        tokens,
        tokens,
        vector,
        vector,
        matrix,
        vector,
        matrix,
        vector,
        vector,
        vector,
        matrix,
        vector,
        matrix,
        vector,
    )
    out_specs = (
        tokens,
        tokens,
        vector,
        vector,
        matrix,
        vector,
        matrix,
        vector,
        vector,
        vector,
        matrix,
        vector,
        matrix,
        vector,
    )
    local = make_local(mesh.shape["dp"], mesh.shape["seq"])
    return jax.shard_map(
        local, mesh=mesh, in_specs=in_specs, out_specs=out_specs, check_vma=False
    )
```

time: 1630 us -> 961 us (0.59)
  waiting for transfers between devices: 1210 us -> 690 us
  blocking collectives: 167 us -> 8.48 us
  matrix products: 167 us -> 87.6 us
  local copies, waits for them, and re-layouts: 32.8 us -> 102 us
    reduce_scatter x4, waiting for transfers between devices: 601 us -> 103 us  [scatter_dp(): return lax.psum_scatter(rows, 'dp', scatter_dimension=0, tiled=True)]
    psum x1, waiting for transfers between devices: 308 us -> 107 us  [local(): small = lax.psum(small, ('dp', 'seq'))]
    all_gather x4 -> x10, waiting for transfers between devices: 261 us -> 364 us  [the longest x6 241 us: gather_seq(): return lax.all_gather(shard, 'seq', axis=0, tiled=False)]
    all_to_all x2 -> x4, waiting for transfers between devices: 32.4 us -> 113 us  [the longest x2 82.1 us: exchange_sum(): got = lax.all_to_all(slabs, 'seq', split_axis=0, concat_axis=0, tiled=True)]
    dot_general x18, matrix products: 167 us -> 87.6 us  [the longest x12 82.6 us: dot(): lax.dot_general(a, b, (contract, ((), ())), preferred_element_type=jnp.fl...]
    all_gather x8 -> x1, blocking collectives: 71.1 us -> 8.48 us  [local(): gathered = lax.all_gather(packed, 'dp', axis=0, tiled=False)]
    all_to_all x2 -> x0, blocking collectives: 56.2 us -> none  [the longest x1 39.6 us: local(): lax.all_to_all(triple_heads, 'seq', split_axis=1, concat_axis=3, tiled=True)]
    convert_element_type x4 -> x7, local copies, waits for them, and re-layouts: 8.63 us -> 49.4 us  [the longest x3 27.3 us: local(): up_full = up_part.reshape(n_seq, own, n_dp, unit).transpose(1, 2, 0, 3).r...]
  transfers between devices with their start and end apart: 11 -> 19, of which waited for: 9 -> 17; matrix products, arithmetic and copies ran while one was open for 13% -> 22% of each run, Pallas kernels for 0% -> 0%
where the time goes in v1:
time: 961 us; the launch traced here: 956 us
  waiting for transfers between devices  690 us (72%)
  local copies, waits for them, and re-layouts  102 us (11%)
  matrix products  87.6 us (9%)
  other arithmetic  33.9 us (4%)
  starting transfers between devices  19 us (2%)
  between operations  15.1 us (2%)
    all_gather x6, waiting for transfers between devices, gather_seq(): return lax.all_gather(shard, 'seq', axis=0, tiled=False)  241 us
    psum x1, waiting for transfers between devices, local(): small = lax.psum(small, ('dp', 'seq'))  107 us
    reduce_scatter x4, waiting for transfers between devices, scatter_dp(): return lax.psum_scatter(rows, 'dp', scatter_dimension=0, tiled=True)  103 us
    all_gather x3, waiting for transfers between devices, gather_dp(): return lax.all_gather(rows, 'dp', axis=0, tiled=True)  102 us
    dot_general x12, matrix products, dot(): lax.dot_general(a, b, (contract, ((), ())), preferred_element_type=jnp.fl...  82.6 us
    all_to_all x2, waiting for transfers between devices, exchange_sum(): got = lax.all_to_all(slabs, 'seq', split_axis=0, concat_axis=0, tiled=True)  82.1 us
    unnamed x131, local copies, waits for them, and re-layouts  27.6 us
    convert_element_type x3, local copies, waits for them, and re-layouts, local(): up_full = up_part.reshape(n_seq, own, n_dp, unit).transpose(1, 2, 0, 3).r...  27.3 us
  transfers between devices with their start and end apart: 19, of which 17 were waited for; matrix products, arithmetic and copies ran while one was open for 22% of the time, Pallas kernels for 0%

profile of v1, /device:TPU:0, one launch (start us, length us, event | category | flops | bytes accessed | tf_op | source)
XLA Modules:
  0.0 955.7 jit_solution(7400377994347457688)
XLA Ops:
  13.3 15.4 %all-to-all-done = bf16[8,32,2048]{2,1,0:T(8,128)(2,1)} async-done(((bf16[8,32,2048]{2,1,0:T(8,128)(2,1)}), bf16[8,32,2048]{2,1,0:T(8,128)(2,1)}, u32[]{:S(2)}, u32[]{:S(2)}) %all-to-all-start) | async-done | bytes 1048608 | tf_op jit(solution)/shard_map/all_to_all | solution.py:102
  34.5 6.4 copy.92
  46.0 8.5 all-gather.6
  64.9 21.6 %all-gather.28.cloned.1.call-done = bf16[16,32,2048]{2,1,0:T(8,128)(2,1)} async-done(((bf16[2,32,2048]{2,1,0:T(8,128)(2,1)}), bf16[16,32,2048]{2,1,0:T(8,128)(2,1)}) %all-gather.28.cloned.1.call-update) | async-done | bytes 2097168 | tf_op jit(solution)/shard_map/all_gather | solution.py:107
  88.2 45.5 %all-gather.26.cloned.1.call-done = bf16[4,128,2048]{2,1,0:T(8,128)(2,1)} async-done(((bf16[1,128,2048]{2,1,0:T(8,128)(2,1)}), bf16[4,128,2048]{2,1,0:T(8,128)(2,1)}) %all-gather.26.cloned.1.call-update) | async-done | bytes 2097168 | tf_op jit(solution)/shard_map/all_gather | solution.py:50
  137.4 42.8 %all-gather.20.cloned.1.call-done = bf16[2048,1536]{1,0:T(8,128)(2,1)} async-done(((bf16[256,1536]{1,0:T(8,128)(2,1)}), bf16[2048,1536]{1,0:T(8,128)(2,1)}) %all-gather.20.cloned.1.call-update) | async-done | bytes 6291472 | tf_op jit(solution)/shard_map/all_gather | solution.py:46
  180.3 8.5 convolution_add_fusion
  218.8 8.2 convolution_convert_fusion.2
  227.1 11.4 %all-gather.22.cloned.1.call-done = bf16[2048,2048]{0,1:T(8,128)(2,1)} async-done(((bf16[256,2048]{0,1:T(8,128)(2,1)}), bf16[2048,2048]{0,1:T(8,128)(2,1)}) %all-gather.22.cloned.1.call-update) | async-done | bytes 8388624 | tf_op jit(solution)/shard_map/all_gather | solution.py:46
  238.5 8.9 multiply_convert_fusion
  247.4 47.7 %all-gather.24.cloned.1.call-done = bf16[2048,2048]{1,0:T(8,128)(2,1)} async-done(((bf16[256,2048]{1,0:T(8,128)(2,1)}), bf16[2048,2048]{1,0:T(8,128)(2,1)}) %all-gather.24.cloned.1.call-update) | async-done | bytes 8388624 | tf_op jit(solution)/shard_map/all_gather | solution.py:46
  295.1 10.7 %fusion.43 = (f32[2048]{0:T(1024)S(1)}, bf16[512,2048]{1,0:T(8,128)(2,1)S(1)}) fusion(f32[512,2048]{1,0:T(8,128)} %get-tuple-element.92, f32[2048]{0:T(1024)S(1)} %bitcast.207, bf16[2048,2048]{1,0:T(8,128)(2,1)} %all-gather.24.cloned.1.call-done, bf16[512,2048]{1,0:T(8,128)(2,1)} %bitcast.216), kind=kOutput, calls=%fused_computation.142 | convolution fusion | flops 4307548160 | bytes 16793600 | tf_op jit(solution)/shard_map/dot_general | solution.py:15
  307.1 6.8 convolution_convert_fusion.1
  315.5 8.5 convolution_convert_fusion
  331.3 10.5 %fusion.38 = (f32[2048]{0:T(1024)S(1)}, f32[2048]{0:T(1024)S(1)}, bf16[512,2048]{1,0:T(8,128)(2,1)}, f32[2048]{0:T(1024)S(1)}, f32[2048]{0:T(1024)S(1)}) fusion(f32[512]{0:T(512)S(1)} %copy-done.36, f32[512]{0:T(512)S(1)} %copy-done.34, bf16[4,128,2048]{2,1,0:T(8,128)(2,1)S(1)} %copy-done.1, f32[2048]{0:T(1024)S(1)} %bitcast.200, ...), kind=kOutput, calls=%fused_computation.137 | convolution fusion | flops 4308590592 | bytes 18927616 | tf_op jit(solution)/shard_map/dot_general | solution.py:15
  346.5 7.1 fusion.44
  356.2 39.2 %all-to-all-done.2 = bf16[4,128,2048]{2,1,0:T(8,128)(2,1)} async-done(((bf16[4,128,2048]{2,1,0:T(8,128)(2,1)}), bf16[4,128,2048]{2,1,0:T(8,128)(2,1)}, u32[]{:S(2)}, u32[]{:S(2)}) %all-to-all-start.2) | async-done | bytes 2097184 | tf_op jit(solution)/shard_map/all_to_all | solution.py:59
  404.9 43.0 %all-to-all-done.1 = bf16[4,128,2048]{2,1,0:T(8,128)(2,1)} async-done(((bf16[4,128,2048]{2,1,0:T(8,128)(2,1)}), bf16[4,128,2048]{2,1,0:T(8,128)(2,1)}, u32[]{:S(2)}, u32[]{:S(2)}) %all-to-all-start.1) | async-done | bytes 2097184 | tf_op jit(solution)/shard_map/all_to_all | solution.py:59
  453.3 27.5 %reduce-scatter.9.cloned.1.call-done = bf16[256,2048]{1,0:T(8,128)(2,1)} async-done(((bf16[2048,2048]{1,0:T(8,128)(2,1)}), bf16[256,2048]{1,0:T(8,128)(2,1)}) %reduce-scatter.9.cloned.1.call-update) | async-done | bytes 1048592 | tf_op jit(solution)/shard_map/reduce_scatter | solution.py:54
  480.9 75.3 %reduce-scatter.11.cloned.1.call-done = bf16[256,2048]{1,0:T(8,128)(2,1)} async-done(((bf16[2048,2048]{1,0:T(8,128)(2,1)}), bf16[256,2048]{1,0:T(8,128)(2,1)}) %reduce-scatter.11.cloned.1.call-update) | async-done | bytes 1048592 | tf_op jit(solution)/shard_map/reduce_scatter | solution.py:54
  556.3 29.6 %all-gather.32.cloned.1.call-done = bf16[256,2048]{1,0:T(8,128)(2,1)} async-done(((bf16[64,2048]{1,0:T(8,128)(2,1)}), bf16[256,2048]{1,0:T(8,128)(2,1)}) %all-gather.32.cloned.1.call-update) | async-done | bytes 1048592 | tf_op jit(solution)/shard_map/all_gather | solution.py:50
  589.7 15.5 %all-to-all-done.3 = bf16[8,32,2048]{2,1,0:T(8,128)(2,1)S(1)} async-done(((bf16[8,32,2048]{2,1,0:T(8,128)(2,1)}), bf16[8,32,2048]{2,1,0:T(8,128)(2,1)S(1)}, u32[]{:S(2)}, u32[]{:S(2)}) %all-to-all-start.3) | async-done | bytes 1048608 | tf_op jit(solution)/shard_map/all_to_all | solution.py:220
  606.9 107.3 %all-reduce.2.cloned.1.call-done = f32[8,3072]{1,0:T(8,128)} async-done(((f32[8,3072]{1,0:T(8,128)}), f32[8,3072]{1,0:T(8,128)}) %all-reduce.2.cloned.1.call-update) | async-done | bytes 98320 | tf_op jit(solution)/shard_map/psum | solution.py:254
  718.5 61.7 %all-gather.30.cloned.1.call-done = bf16[1024,1536]{1,0:T(8,128)(2,1)} async-done(((bf16[256,1536]{1,0:T(8,128)(2,1)}), bf16[1024,1536]{1,0:T(8,128)(2,1)}) %all-gather.30.cloned.1.call-update) | async-done | bytes 3145744 | tf_op jit(solution)/shard_map/all_gather | solution.py:50
  785.6 8.2 reshape.417
  793.8 6.6 copy.106
  800.4 6.6 copy.109
  806.9 54.1 %all-gather.34.cloned.1.call-done = bf16[1024,2048]{1,0:T(8,128)(2,1)} async-done(((bf16[256,2048]{1,0:T(8,128)(2,1)}), bf16[1024,2048]{1,0:T(8,128)(2,1)}) %all-gather.34.cloned.1.call-update) | async-done | bytes 4194320 | tf_op jit(solution)/shard_map/all_gather | solution.py:50
  869.5 12.4 %copy.108 = f32[256,8,4,256]{3,2,1,0:T(4,128)} copy(f32[256,8,4,256]{3,1,0,2:T(8,128)} %bitcast_bitcast_fusion) | data formatting | bytes 16777216 | tf_op jit(solution)/shard_map/convert_element_type | solution.py:211
  881.9 10.7 %reshape.415 = f32[256,8192]{1,0:T(8,128)} reshape(f32[256,8,4,256]{3,2,1,0:T(4,128)} %copy.108) | data formatting | bytes 16777216 | tf_op jit(solution)/shard_map/convert_element_type | solution.py:211
  892.6 49.1 %all-gather.36.cloned.1.call-done = bf16[1024,2048]{1,0:T(8,128)(2,1)} async-done(((bf16[256,2048]{1,0:T(8,128)(2,1)}), bf16[1024,2048]{1,0:T(8,128)(2,1)}) %all-gather.36.cloned.1.call-update) | async-done | bytes 4194320 | tf_op jit(solution)/shard_map/all_gather | solution.py:50
  941.7 6.7 convert_element_type.310
  (247 shorter events, 118.6 us)
Async XLA Ops:
  7.2 24.1 %copy-start.12 = (bf16[256,6144]{1,0:T(8,128)(2,1)S(1)}, bf16[256,6144]{1,0:T(8,128)(2,1)}, u32[]{:S(2)}) copy-start(bf16[256,6144]{1,0:T(8,128)(2,1)} %param.18) | copy-start | bytes 9437188
  7.2 50.8 %all-gather.18.cloned.1.call-start = ((), (), s32[]{:S(2)}) async-start(), calls=%async_computation.8 | async-start | bytes 2621440 | tf_op jit(solution)/shard_map/all_gather | solution.py:50
  7.9 20.8 %all-to-all-start = ((bf16[8,32,2048]{2,1,0:T(8,128)(2,1)}), bf16[8,32,2048]{2,1,0:T(8,128)(2,1)}, u32[]{:S(2)}, u32[]{:S(2)}) async-start(bf16[8,32,2048]{2,1,0:T(8,128)(2,1)} %bitcast.187), calls=%async_computation | async-start | bytes 2097152 | tf_op jit(solution)/shard_map/all_to_all | solution.py:102
  13.3 73.2 %all-gather.28.cloned.1.call-start = ((), (), s32[]{:S(2)}) async-start(), calls=%async_computation.18 | async-start | bytes 2359296 | tf_op jit(solution)/shard_map/all_gather | solution.py:107
  30.4 103.3 %all-gather.26.cloned.1.call-start = ((), (), s32[]{:S(2)}) async-start(), calls=%async_computation.12 | async-start | bytes 2621440 | tf_op jit(solution)/shard_map/all_gather | solution.py:50
  31.2 149.1 %all-gather.20.cloned.1.call-start = ((), (), s32[]{:S(2)}) async-start(), calls=%async_computation.9 | async-start | bytes 7077888 | tf_op jit(solution)/shard_map/all_gather | solution.py:46
  34.5 204.0 %all-gather.22.cloned.1.call-start = ((), (), s32[]{:S(2)}) async-start(), calls=%async_computation.10 | async-start | bytes 9437184 | tf_op jit(solution)/shard_map/all_gather | solution.py:46
  43.3 251.8 %all-gather.24.cloned.1.call-start = ((), (), s32[]{:S(2)}) async-start(), calls=%async_computation.11 | async-start | bytes 9437184 | tf_op jit(solution)/shard_map/all_gather | solution.py:46
  45.7 356.4 %reduce-scatter.7.cloned.1.call-start = ((), (), s32[]{:S(2)}) async-start(), calls=%async_computation.15 | async-start | bytes 2359296 | tf_op jit(solution)/shard_map/reduce_scatter | solution.py:54
  88.2 49.2 %copy-start.6 = (bf16[2,8,32,2048]{3,2,1,0:T(8,128)(2,1)}, bf16[2,8,32,2048]{3,2,1,0:T(8,128)(2,1)S(1)}, u32[]{:S(2)}) copy-start(bf16[2,8,32,2048]{3,2,1,0:T(8,128)(2,1)S(1)} %copy.91) | copy-start | bytes 6291460
  205.0 247.6 %reduce-scatter.5.cloned.1.call-start = ((), (), s32[]{:S(2)}) async-start(), calls=%async_computation.14 | async-start | bytes 7077888 | tf_op jit(solution)/shard_map/reduce_scatter | solution.py:54
  227.0 11.5 %copy-start.19 = (bf16[512,2048]{1,0:T(8,128)(2,1)S(1)}, bf16[512,2048]{1,0:T(8,128)(2,1)}, u32[]{:S(2)}) copy-start(bf16[512,2048]{1,0:T(8,128)(2,1)} %get-tuple-element.54) | copy-start | bytes 6291460
  227.0 253.8 %reduce-scatter.9.cloned.1.call-start = ((), (), s32[]{:S(2)}) async-start(), calls=%async_computation.16 | async-start | bytes 9437184 | tf_op jit(solution)/shard_map/reduce_scatter | solution.py:54
  313.9 242.3 %reduce-scatter.11.cloned.1.call-start = ((), (), s32[]{:S(2)}) async-start(), calls=%async_computation.17 | async-start | bytes 9437184 | tf_op jit(solution)/shard_map/reduce_scatter | solution.py:54
  325.4 5.8 copy-start.1
  325.4 5.8 copy-start.34
  325.4 5.8 copy-start.36
  325.4 5.8 copy-start.50
  341.8 53.6 %all-to-all-start.2 = ((bf16[4,128,2048]{2,1,0:T(8,128)(2,1)}), bf16[4,128,2048]{2,1,0:T(8,128)(2,1)}, u32[]{:S(2)}, u32[]{:S(2)}) async-start(bf16[4,128,2048]{2,1,0:T(8,128)(2,1)} %bitcast.31), calls=%async_computation.2 | async-start | bytes 4194304 | tf_op jit(solution)/shard_map/all_to_all | solution.py:59
  346.5 7.1 copy-start.7
  346.5 7.1 copy-start.11
  356.2 43.8 %copy-start.2 = (bf16[1,128,2048]{2,1,0:T(8,128)(2,1)S(1)}, bf16[1,128,2048]{2,1,0:T(8,128)(2,1)}, u32[]{:S(2)}) copy-start(bf16[1,128,2048]{2,1,0:T(8,128)(2,1)} %param.14) | copy-start | bytes 1572868
  356.2 44.3 %copy-start.4 = (f32[512,1,2,256]{3,0,2,1:T(8,128)S(1)}, f32[512,1,2,256]{3,0,2,1:T(8,128)}, u32[]{:S(2)}) copy-start(f32[512,1,2,256]{3,0,2,1:T(8,128)} %copy-done.3) | copy-start | bytes 3145732
  395.4 52.4 %all-to-all-start.1 = ((bf16[4,128,2048]{2,1,0:T(8,128)(2,1)}), bf16[4,128,2048]{2,1,0:T(8,128)(2,1)}, u32[]{:S(2)}, u32[]{:S(2)}) async-start(bf16[4,128,2048]{2,1,0:T(8,128)(2,1)} %bitcast.15), calls=%async_computation.1 | async-start | bytes 4194304 | tf_op jit(solution)/shard_map/all_to_all | solution.py:59
  399.9 186.0 %all-gather.32.cloned.1.call-start = ((), (), s32[]{:S(2)}) async-start(), calls=%async_computation.20 | async-start | bytes 1310720 | tf_op jit(solution)/shard_map/all_gather | solution.py:50
  402.1 312.1 %all-reduce.2.cloned.1.call-start = ((), (), s32[]{:S(2)}) async-start(), calls=%async_computation.13 | async-start | bytes 196608 | tf_op jit(solution)/shard_map/psum | solution.py:254
  404.5 45.4 %copy-start.13 = (bf16[1,128,2048]{2,1,0:T(8,128)(2,1)S(1)}, bf16[1,128,2048]{2,1,0:T(8,128)(2,1)}, u32[]{:S(2)}) copy-start(bf16[1,128,2048]{2,1,0:T(8,128)(2,1)} %param.15) | copy-start | bytes 1572868
  452.5 327.7 %all-gather.30.cloned.1.call-start = ((), (), s32[]{:S(2)}) async-start(), calls=%async_computation.19 | async-start | bytes 3932160 | tf_op jit(solution)/shard_map/all_gather | solution.py:50
  453.3 407.8 %all-gather.34.cloned.1.call-start = ((), (), s32[]{:S(2)}) async-start(), calls=%async_computation.21 | async-start | bytes 5242880 | tf_op jit(solution)/shard_map/all_gather | solution.py:50
  480.9 460.8 %all-gather.36.cloned.1.call-start = ((), (), s32[]{:S(2)}) async-start(), calls=%async_computation.22 | async-start | bytes 5242880 | tf_op jit(solution)/shard_map/all_gather | solution.py:50
  585.8 19.4 %all-to-all-start.3 = ((bf16[8,32,2048]{2,1,0:T(8,128)(2,1)}), bf16[8,32,2048]{2,1,0:T(8,128)(2,1)S(1)}, u32[]{:S(2)}, u32[]{:S(2)}) async-start(bf16[8,32,2048]{2,1,0:T(8,128)(2,1)} %bitcast.188), calls=%async_computation.5 | async-start | bytes 2097152 | tf_op jit(solution)/shard_map/all_to_all | solution.py:220
  715.6 232.7 %copy-start.37 = (f32[1,256]{1,0:T(1,128)}, f32[1,256]{1,0:T(1,128)S(1)}, u32[]{:S(2)}) copy-start(f32[1,256]{1,0:T(1,128)S(1)} %get-tuple-element.77) | copy-start | bytes 3076
  (38 other events, 93.0 us)
Sparse Core Ops, SparseCore 0:
  9.6 48.3 all-gather.17
  59.9 26.5 all-gather.27
  88.1 45.6 all-gather.25
  136.1 44.1 all-gather.19
  182.6 55.8 all-gather.21
  240.8 54.2 all-gather.23
  298.4 41.1 reduce-scatter.6
  343.5 61.7 reduce-scatter.4
  409.3 71.4 reduce-scatter.8
  484.7 71.4 reduce-scatter.10
  557.8 27.9 all-gather.31
  591.3 122.9 all-reduce.1
  715.8 64.3 all-gather.29
  781.6 79.3 all-gather.33
  862.4 79.2 all-gather.35

commit v2 on v1

--- a/solution.py
+++ b/solution.py
@@ -1,6 +1,10 @@
+import functools
+
 import jax
 import jax.numpy as jnp
 from jax import lax
+from jax.experimental import pallas as pl
+from jax.experimental.pallas import tpu as pltpu
 from jax.sharding import PartitionSpec as P
 
 H = 8
@@ -9,6 +13,435 @@
 
 epsilon = 1e-05
 masked_fill = -1e30
+
+MESH = pl.DeviceIdType.MESH
+
+
+def bits_of(n):
+    return n.bit_length() - 1
+
+
+def flipped(me, mask):
+    for k in range(mask.bit_length()):
+        if mask >> k & 1:
+            me = me + (1 << k) * (1 - 2 * ((me // (1 << k)) % 2))
+    return me
+
+
+def chip_orders(n):
+    chips = [1 << k for k in range(1, bits_of(n))]
+    return chips, chips[1:] + chips[:1]
+
+
+def greet(n_dp, n_seq, me, z, along_seq):
+    barrier = pltpu.get_barrier_semaphore()
+    peers = bits_of(n_dp)
+    for k in range(bits_of(n_dp)):
+        pl.semaphore_signal(
+            barrier, inc=1, device_id={"dp": flipped(me, 1 << k)}, device_id_type=MESH
+        )
+    if along_seq:
+
+        @pl.when(z > 0)
+        def _():
+            pl.semaphore_signal(barrier, inc=1, device_id={"seq": z - 1}, device_id_type=MESH)
+
+        @pl.when(z < n_seq - 1)
+        def _():
+            pl.semaphore_signal(barrier, inc=1, device_id={"seq": z + 1}, device_id_type=MESH)
+
+        peers = peers + (z + n_seq - 1) // n_seq + (2 * n_seq - 2 - z) // n_seq
+    pl.semaphore_wait(barrier, peers)
+
+
+class Spread:
+    def __init__(self, n_dp, me, own, out, send_sem, recv_sem):
+        self.n_dp, self.me, self.own, self.out = n_dp, me, own, out
+        self.send_sem, self.recv_sem = send_sem, recv_sem
+        self.half = own.shape[0] // 2
+        self.orders = [list(order) + [1] for order in chip_orders(n_dp)]
+
+    def copy(self, color, piece, bit):
+        rows = pl.ds(color * self.half, self.half)
+        owner = flipped(self.me, piece)
+        source = self.own.at[rows] if piece == 0 else self.out.at[owner, rows]
+        return pltpu.make_async_remote_copy(
+            src_ref=source,
+            dst_ref=self.out.at[owner, rows],
+            send_sem=self.send_sem.at[color, piece | bit],
+            recv_sem=self.recv_sem.at[color, piece | bit],
+            device_id={"dp": flipped(self.me, bit)},
+            device_id_type=MESH,
+        )
+
+    def later(self, color, piece):
+        order = self.orders[color]
+        last = max((order.index(b) for b in order if piece & b), default=-1)
+        return order[last + 1 :]
+
+    def start(self, color, piece):
+        for bit in self.later(color, piece):
+            self.copy(color, piece, bit).start()
+
+    def arrivals(self, color):
+        pieces = [0]
+        for bit in self.orders[color]:
+            pieces += [p | bit for p in pieces]
+        return pieces[1:]
+
+    def last_bit(self, color, piece):
+        order = self.orders[color]
+        return order[max(order.index(b) for b in order if piece & b)]
+
+    def receive(self, color, piece):
+        bit = self.last_bit(color, piece)
+        rows = pl.ds(color * self.half, self.half)
+        owner = flipped(self.me, piece)
+        pltpu.make_async_remote_copy(
+            src_ref=self.out.at[owner, rows],
+            dst_ref=self.out.at[owner, rows],
+            send_sem=self.send_sem.at[color, piece],
+            recv_sem=self.recv_sem.at[color, piece],
+            device_id={"dp": flipped(self.me, bit)},
+            device_id_type=MESH,
+        ).wait_recv()
+
+    def drain(self):
+        for color in range(2):
+            for piece in range(self.n_dp):
+                for bit in self.later(color, piece):
+                    self.copy(color, piece, bit).wait_send()
+
+
+class Chain:
+    def __init__(self, n_seq, z, own, out, send_sem, recv_sem):
+        self.n_seq, self.z, self.own, self.out = n_seq, z, own, out
+        self.send_sem, self.recv_sem = send_sem, recv_sem
+
+    def copy(self, way, k):
+        shard = self.z - k if way == 0 else self.z + k
+        source = self.own if k == 0 else self.out.at[shard]
+        return pltpu.make_async_remote_copy(
+            src_ref=source,
+            dst_ref=self.out.at[shard],
+            send_sem=self.send_sem.at[way, k],
+            recv_sem=self.recv_sem.at[way, k],
+            device_id={"seq": self.z + 1 if way == 0 else self.z - 1},
+            device_id_type=MESH,
+        )
+
+    def arrived(self, way, k):
+        shard = self.z - k if way == 0 else self.z + k
+        return pltpu.make_async_remote_copy(
+            src_ref=self.out.at[shard],
+            dst_ref=self.out.at[shard],
+            send_sem=self.send_sem.at[way, k - 1],
+            recv_sem=self.recv_sem.at[way, k - 1],
+            device_id={"seq": self.z - 1 if way == 0 else self.z + 1},
+            device_id_type=MESH,
+        )
+
+    def has(self, way, k):
+        return self.z >= k if way == 0 else self.z + k <= self.n_seq - 1
+
+    def more(self, way):
+        return self.z < self.n_seq - 1 if way == 0 else self.z > 0
+
+    def start(self, k):
+        for way in range(2):
+
+            @pl.when(jnp.logical_and(self.has(way, k), self.more(way)))
+            def _():
+                self.copy(way, k).start()
+
+    def receive(self, k):
+        for way in range(2):
+
+            @pl.when(self.has(way, k))
+            def _():
+                self.arrived(way, k).wait_recv()
+
+            if k < self.n_seq - 1:
+
+                @pl.when(jnp.logical_and(self.has(way, k), self.more(way)))
+                def _():
+                    self.copy(way, k).start()
+
+    def drain(self):
+        for k in range(self.n_seq - 1):
+            for way in range(2):
+
+                @pl.when(jnp.logical_and(self.has(way, k), self.more(way)))
+                def _():
+                    self.copy(way, k).wait_send()
+
+
+def fetch_kernel(n_dp, n_seq, unit, *refs):
+    (x_ref, c_ref, p_ref, up_ref, down_ref) = refs[:5]
+    (x_out, c_out, p_out, up_out, down_out) = refs[5:10]
+    (up_own, down_own, load_sem, keep_sem, zs, zr, ds, dr) = refs[10:]
+    me, z = lax.axis_index("dp"), lax.axis_index("seq")
+    ff_own = unit * n_seq
+    if up_ref.shape == up_own.shape:
+        loads = [pltpu.make_async_copy(up_ref, up_own, load_sem.at[0])]
+    else:
+        loads = [
+            pltpu.make_async_copy(
+                up_ref.at[:, pl.ds(pl.multiple_of(d * ff_own + z * unit, 128), unit)],
+                up_own.at[:, pl.ds(d * unit, unit)],
+                load_sem.at[d],
+            )
+            for d in range(n_dp)
+        ]
+    loads.append(
+        pltpu.make_async_copy(
+            down_ref.at[pl.ds(pl.multiple_of(z * unit, 16), unit)], down_own, load_sem.at[n_dp]
+        )
+    )
+    for load in loads:
+        load.start()
+    greet(n_dp, n_seq, me, z, True)
+    chains = [
+        Chain(n_seq, z, own, out, zs.at[i], zr.at[i])
+        for i, (own, out) in enumerate(((x_ref, x_out), (c_ref, c_out)))
+    ]
+    spreads = [
+        Spread(n_dp, me, own, out, ds.at[i], dr.at[i])
+        for i, (own, out) in enumerate(((p_ref, p_out), (up_own, up_out), (down_own, down_out)))
+    ]
+    for chain in chains:
+        chain.start(0)
+    for color in range(2):
+        spreads[0].start(color, 0)
+    for load in loads[:-1]:
+        load.wait()
+    for color in range(2):
+        spreads[1].start(color, 0)
+    loads[-1].wait()
+    for color in range(2):
+        spreads[2].start(color, 0)
+    keeps = [
+        pltpu.make_async_copy(own, out.at[at], keep_sem.at[i])
+        for i, (own, out, at) in enumerate(
+            (
+                (x_ref, x_out, z),
+                (c_ref, c_out, z),
+                (p_ref, p_out, me),
+                (up_own, up_out, me),
+                (down_own, down_out, me),
+            )
+        )
+    ]
+    for keep in keeps:
+        keep.start()
+    work = []
+    for i, spread in enumerate(spreads):
+        lists = [spread.arrivals(color) for color in range(2)]
+        for at, pair in enumerate(zip(*lists)):
+            for color, piece in enumerate(pair):
+                when = (piece & ~1).bit_count() + 0.1 * i + 0.5 * (piece & 1)
+                work.append((when, at, i, color, piece))
+    work.sort()
+    rounds = sorted({int(item[0]) for item in work})
+    step = 1
+    for stage in rounds:
+        if step < n_seq:
+            for chain in chains:
+                chain.receive(step)
+            step += 1
+        for _, _, i, color, piece in [w for w in work if int(w[0]) == stage]:
+            spreads[i].receive(color, piece)
+            spreads[i].start(color, piece)
+    while step < n_seq:
+        for chain in chains:
+            chain.receive(step)
+        step += 1
+    for keep in keeps:
+        keep.wait()
+    for chain in chains:
+        chain.drain()
+    for spread in spreads:
+        spread.drain()
+
+
+def fetch(n_dp, n_seq, unit, x, c, params, w_up, w_down):
+    rows, width = x.shape
+    own = w_up.shape[0]
+    if unit % 128:
+        w_up = lax.dynamic_index_in_dim(
+            w_up.reshape(own, n_dp, n_seq, unit), lax.axis_index("seq"), 2, keepdims=False
+        ).reshape(own, n_dp * unit)
+    anywhere = pl.BlockSpec(memory_space=pl.ANY)
+    inside = pl.BlockSpec(memory_space=pltpu.VMEM)
+    return pl.pallas_call(
+        functools.partial(fetch_kernel, n_dp, n_seq, unit),
+        out_shape=(
+            jax.ShapeDtypeStruct((n_seq, rows, width), x.dtype),
+            jax.ShapeDtypeStruct((n_seq, rows, width), x.dtype),
+            jax.ShapeDtypeStruct((n_dp, *params.shape), params.dtype),
+            jax.ShapeDtypeStruct((n_dp, own, n_dp * unit), w_up.dtype),
+            jax.ShapeDtypeStruct((n_dp, unit, width), w_down.dtype),
+        ),
+        in_specs=[inside, inside, inside, anywhere, anywhere],
+        out_specs=(anywhere,) * 5,
+        scratch_shapes=[
+            pltpu.VMEM((own, n_dp * unit), w_up.dtype),
+            pltpu.VMEM((unit, width), w_down.dtype),
+            pltpu.SemaphoreType.DMA((n_dp + 1,)),
+            pltpu.SemaphoreType.DMA((5,)),
+            pltpu.SemaphoreType.DMA((2, 2, n_seq)),
+            pltpu.SemaphoreType.DMA((2, 2, n_seq)),
+            pltpu.SemaphoreType.DMA((3, 2, n_dp)),
+            pltpu.SemaphoreType.DMA((3, 2, n_dp)),
+        ],
+        compiler_params=pltpu.CompilerParams(collective_id=0, has_side_effects=True),
+        cost_estimate=pl.CostEstimate(flops=0, bytes_accessed=200_000_000, transcendentals=0),
+        name="fetch",
+    )(x, c, params, w_up, w_down)
+
+
+def reduce_kernel(n_dp, n_seq, shapes, *refs):
+    count = len(shapes)
+    grads, outs = refs[:count], refs[count : 2 * count]
+    scratch = refs[2 * count :]
+    me, z = lax.axis_index("dp"), lax.axis_index("seq")
+    bits = bits_of(n_dp)
+    orders = chip_orders(n_dp)
+    greet(n_dp, n_seq, me, z, False)
+
+    for i in range(count):
+        grad, out = grads[i], outs[i]
+        mine, first, load_sem, s0, r0, *stages = scratch[i * (5 + 3 * (bits - 1)) :][
+            : 5 + 3 * (bits - 1)
+        ]
+        half = shapes[i][0] // n_dp // 2
+
+        def rows_of(color, dest):
+            return pl.ds(pl.multiple_of((flipped(me, dest) * 2 + color) * half, 8), half)
+
+        def core_copy(color, dest):
+            return pltpu.make_async_remote_copy(
+                src_ref=grad.at[rows_of(color, dest | 1)],
+                dst_ref=first.at[color, dest // 2],
+                send_sem=s0.at[color, dest // 2],
+                recv_sem=r0.at[color, dest // 2],
+                device_id={"dp": flipped(me, 1)},
+                device_id_type=MESH,
+            )
+
+        def own_load(color, dest):
+            return pltpu.make_async_copy(
+                grad.at[rows_of(color, dest)], mine.at[color, dest // 2], load_sem.at[color, dest // 2]
+            )
+
+        def ranked(color):
+            order = orders[color]
+
+            def key(dest):
+                return tuple(0 if dest & bit else 1 for bit in order)
+
+            return sorted(range(0, n_dp, 2), key=key)
+
+        for dests in zip(ranked(0), ranked(1)):
+            for color, dest in enumerate(dests):
+                core_copy(color, dest).start()
+                own_load(color, dest).start()
+
+        def stage_copy(color, stage, dest):
+            bit = orders[color][stage]
+            land, ss, rr = stages[3 * stage : 3 * stage + 3]
+            return pltpu.make_async_remote_copy(
+                src_ref=mine.at[color, dest // 2],
+                dst_ref=land.at[color, slot(color, stage, dest & ~bit)],
+                send_sem=ss.at[color, slot(color, stage, dest & ~bit)],
+                recv_sem=rr.at[color, slot(color, stage, dest & ~bit)],
+                device_id={"dp": flipped(me, bit)},
+                device_id_type=MESH,
+            )
+
+        def slot(color, stage, dest):
+            rest = orders[color][stage + 1 :]
+            return sum(1 << k for k, bit in enumerate(rest) if dest & bit)
+
+        def add(color, dest, other, target):
+            block = min(16, half)
+
+            def body(step, carry):
+                at = pl.ds(pl.multiple_of(step * block, block), block)
+                total = mine[color, dest // 2, at, :].astype(jnp.float32) + other[at, :].astype(
+                    jnp.float32
+                )
+                target[at, :] = total.astype(target.dtype)
+                return carry
+
+            lax.fori_loop(0, half // block, body, 0)
+
+        for dests in zip(ranked(0), ranked(1)):
+            for color, dest in enumerate(dests):
+                core_copy(color, dest).wait_recv()
+                own_load(color, dest).wait()
+                add(color, dest, first.at[color, dest // 2], mine.at[color, dest // 2])
+                if dest & orders[color][0]:
+                    stage_copy(color, 0, dest).start()
+        for stage in range(bits - 1):
+            last = stage == bits - 2
+            for dests in zip(ranked(0), ranked(1)):
+                for color, dest in enumerate(dests):
+                    order = orders[color]
+                    if any(dest & bit for bit in order[: stage + 1]):
+                        continue
+                    land = stages[3 * stage]
+                    stage_copy(color, stage, dest | order[stage]).wait_recv()
+                    place = land.at[color, slot(color, stage, dest)]
+                    if last:
+                        add(color, dest, place, out.at[pl.ds(color * half, half)])
+                    else:
+                        add(color, dest, place, mine.at[color, dest // 2])
+                        if dest & order[stage + 1]:
+                            stage_copy(color, stage + 1, dest).start()
+        for color in range(2):
+            for dest in range(0, n_dp, 2):
+                core_copy(color, dest).wait_send()
+                for stage, bit in enumerate(orders[color]):
+                    if dest & bit and not any(dest & b for b in orders[color][:stage]):
+                        stage_copy(color, stage, dest).wait_send()
+
+
+def reduce_rows(n_dp, n_seq, ident, *grads):
+    bits = bits_of(n_dp)
+    anywhere = pl.BlockSpec(memory_space=pl.ANY)
+    inside = pl.BlockSpec(memory_space=pltpu.VMEM)
+    scratch = []
+    for grad in grads:
+        rows, cols = grad.shape
+        half = rows // n_dp // 2
+        kind = grad.dtype
+        scratch += [
+            pltpu.VMEM((2, n_dp // 2, half, cols), kind),
+            pltpu.VMEM((2, n_dp // 2, half, cols), kind),
+            pltpu.SemaphoreType.DMA((2, n_dp // 2)),
+            pltpu.SemaphoreType.DMA((2, n_dp // 2)),
+            pltpu.SemaphoreType.DMA((2, n_dp // 2)),
+        ]
+        for stage in range(bits - 1):
+            left = n_dp // 2 >> (stage + 1)
+            scratch += [
+                pltpu.VMEM((2, left, half, cols), kind),
+                pltpu.SemaphoreType.DMA((2, left)),
+                pltpu.SemaphoreType.DMA((2, left)),
+            ]
+    return pl.pallas_call(
+        functools.partial(reduce_kernel, n_dp, n_seq, tuple(g.shape for g in grads)),
+        out_shape=tuple(
+            jax.ShapeDtypeStruct((g.shape[0] // n_dp, g.shape[1]), g.dtype) for g in grads
+        ),
+        in_specs=[anywhere] * len(grads),
+        out_specs=(inside,) * len(grads),
+        scratch_shapes=scratch,
+        compiler_params=pltpu.CompilerParams(collective_id=ident, has_side_effects=True),
+        cost_estimate=pl.CostEstimate(flops=0, bytes_accessed=100_000_000, transcendentals=0),
+        name=f"reduce_{ident}",
+    )(*grads)
 
 
 def dot(a, b, contract):
@@ -48,10 +481,6 @@
 
 def gather_seq(shard):
     return lax.all_gather(shard, "seq", axis=0, tiled=False)
-
-
-def scatter_dp(rows):
-    return lax.psum_scatter(rows, "dp", scatter_dimension=0, tiled=True)
 
 
 def exchange_sum(partial, n_seq):
@@ -87,12 +516,6 @@
         heads = H // n_seq
         z = lax.axis_index("seq")
 
-        up_own = lax.dynamic_index_in_dim(
-            w_up.reshape(own, n_dp, n_seq, unit), z, 2, keepdims=False
-        ).reshape(own, n_dp * unit)
-        up_w = gather_dp(up_own)
-        down_own = lax.dynamic_slice_in_dim(w_down, z * unit, unit, 0)
-        down_w = gather_dp(down_own)
         qkv_own = lax.dynamic_slice_in_dim(
             w_qkv.reshape(own, 3, H, HD), z * heads, heads, 2
         ).reshape(own, 3 * heads * HD)
@@ -112,7 +535,21 @@
         packed = jnp.concatenate(
             [ln1_gain, ln1_bias, ln2_gain, ln2_bias, b_out, b_down, b_qkv, b_up]
         )
-        gathered = lax.all_gather(packed, "dp", axis=0, tiled=False)
+        packed = jnp.pad(packed, (0, -packed.shape[0] % 2048)).reshape(-1, 128)
+        tokens, incoming, gathered, up_w, down_w = fetch(
+            n_dp,
+            n_seq,
+            unit,
+            layer_input.reshape(tok_local, width),
+            cotangent.reshape(tok_local, width),
+            packed,
+            w_up,
+            w_down,
+        )
+        tokens, incoming = tokens.reshape(length, width), incoming.reshape(length, width)
+        gathered = gathered.reshape(n_dp, -1)
+        up_w = up_w.reshape(width, n_dp * unit)
+        down_w = down_w.reshape(n_dp * unit, width)
         gain_one, shift_one, gain_two, shift_two, out_b, down_b = (
             gathered[:, k * own : (k + 1) * own].reshape(width) for k in range(6)
         )
@@ -121,11 +558,8 @@
             gathered[:, base : base + 3 * own].reshape(3, H, HD), z * heads, heads, 1
         ).reshape(3 * heads * HD)
         up_b = lax.dynamic_index_in_dim(
-            gathered[:, base + 3 * own :].reshape(n_dp, n_seq, unit), z, 1, keepdims=False
+            gathered[:, base + 3 * own : base + 3 * own + ff_own].reshape(n_dp, n_seq, unit), z, 1, keepdims=False
         ).reshape(n_dp * unit)
-
-        tokens = gather_seq(layer_input.reshape(tok_local, width)).reshape(length, width)
-        incoming = gather_seq(cotangent.reshape(tok_local, width)).reshape(length, width)
 
         normed, _ = normalize(tokens.astype(f32))
         mlp_in = (normed * gain_two + shift_two).astype(bf16)
@@ -203,34 +637,6 @@
             - normed_own * jnp.mean(scaled * normed_own, axis=-1, keepdims=True)
         )
 
-        down_part = gather_seq(scatter_dp(down_grad))
-        down_full = down_part.reshape(ff_own, width).astype(f32)
-        up_part = gather_seq(scatter_dp(up_grad))
-        up_full = (
-            up_part.reshape(n_seq, own, n_dp, unit).transpose(1, 2, 0, 3).reshape(own, ff)
-        ).astype(f32)
-        out_part = gather_seq(
-            scatter_dp(
-                out_grad.reshape(owners, n_dp, piece, width)
-                .transpose(1, 0, 2, 3)
-                .reshape(n_dp * owners * piece, width)
-            )
-        )
-        out_full = (
-            lax.all_to_all(
-                out_part.reshape(n_dp, piece, width), "dp", split_axis=0, concat_axis=0, tiled=True
-            )
-            .reshape(own, width)
-            .astype(f32)
-        )
-        qkv_part = gather_seq(scatter_dp(qkv_grad))
-        qkv_full = (
-            qkv_part.reshape(n_seq, own, 3, heads * HD)
-            .transpose(1, 2, 0, 3)
-            .reshape(own, 3 * width)
-            .astype(f32)
-        )
-
         here = jnp.arange(n_seq) == z
         b_up_wide = jnp.where(
             here[None, :, None], b_up_grad.reshape(n_dp, 1, unit), 0.0
@@ -251,11 +657,55 @@
             ],
             axis=1,
         )
-        small = lax.psum(small, ("dp", "seq"))
-        mine = lax.dynamic_index_in_dim(small, lax.axis_index("dp"), 0, keepdims=False)
+        small_len = small.shape[1]
+        small = jnp.pad(small, ((0, 0), (0, -small_len % 4096))).reshape(-1, 256)
+
+        (down_sum,) = reduce_rows(n_dp, n_seq, 1, down_grad)
+        down_full = gather_seq(down_sum).reshape(ff_own, width).astype(f32)
+        (up_sum,) = reduce_rows(n_dp, n_seq, 2, up_grad)
+        up_full = (
+            gather_seq(up_sum)
+            .reshape(n_seq, own, n_dp, unit)
+            .transpose(1, 2, 0, 3)
+            .reshape(own, ff)
+        ).astype(f32)
+        out_sum, small_sum = reduce_rows(
+            n_dp,
+            n_seq,
+            3,
+            out_grad.reshape(owners, n_dp, piece, width)
+            .transpose(1, 0, 2, 3)
+            .reshape(n_dp * owners * piece, width),
+            small,
+        )
+        few = owners * piece
+        small_sum = small_sum.reshape(-1, width).astype(bf16)
+        extra = small_sum.shape[0]
+        tail = jnp.pad(small_sum, ((0, -extra % 16), (0, 0)))
+        out_part = gather_seq(jnp.concatenate([out_sum, tail], axis=0))
+        out_full = (
+            lax.all_to_all(
+                out_part[:, :few].reshape(n_dp, piece, width),
+                "dp",
+                split_axis=0,
+                concat_axis=0,
+                tiled=True,
+            )
+            .reshape(own, width)
+            .astype(f32)
+        )
+        mine = jnp.sum(out_part[:, few : few + extra].astype(f32), axis=0).reshape(-1)
         g1, s1, g2, s2, bd = (mine[k * own : (k + 1) * own] for k in range(5))
         bq = mine[5 * own : 8 * own]
-        bu = mine[8 * own :]
+        bu = mine[8 * own : small_len]
+        (qkv_sum,) = reduce_rows(n_dp, n_seq, 4, qkv_grad)
+        qkv_full = (
+            gather_seq(qkv_sum)
+            .reshape(n_seq, own, 3, heads * HD)
+            .transpose(1, 2, 0, 3)
+            .reshape(own, 3 * width)
+            .astype(f32)
+        )
 
         return (
             output.reshape(layer_input.shape),

time: 961 us -> 632 us (0.66)
  waiting for transfers between devices: 690 us -> 133 us
  Pallas kernels: 0 us -> 242 us
  local copies, waits for them, and re-layouts: 102 us -> 85.2 us
  blocking collectives: 8.48 us -> 18.5 us
    pallas_call x0 -> x5, Pallas kernels: none -> 242 us  [the longest x4 133 us: reduce_rows(): pl.pallas_call(functools.partial(reduce_kernel, n_dp, n_seq, tuple((g.sha...]
    all_gather x6 -> x4, waiting for transfers between devices: 241 us -> 37.2 us  [gather_seq(): return lax.all_gather(shard, 'seq', axis=0, tiled=False)]
    psum x1 -> x0, waiting for transfers between devices: 107 us -> none  [local(): small = lax.psum(small, ('dp', 'seq'))]
    reduce_scatter x4 -> x0, waiting for transfers between devices: 103 us -> none  [scatter_dp(): return lax.psum_scatter(rows, 'dp', scatter_dimension=0, tiled=True)]
    all_gather x3 -> x1, waiting for transfers between devices: 102 us -> 0.01 us  [gather_dp(): return lax.all_gather(rows, 'dp', axis=0, tiled=True)]
    all_gather x1, waiting for transfers between devices: 21.6 us -> 0.01 us  [local(): lax.all_gather(out_own, 'dp', axis=0, tiled=False).transpose(1, 0, 2, 3)]
    all_to_all x0 -> x1, blocking collectives: none -> 18.5 us  [local(): lax.all_to_all(out_part[:, :few].reshape(n_dp, piece, width), 'dp', split...]
    all_to_all x1 -> x0, waiting for transfers between devices: 15.5 us -> none  [local(): lax.all_to_all(out_part.reshape(n_dp, piece, width), 'dp', split_axis=0,...]
  transfers between devices with their start and end apart: 19 -> 9, of which waited for: 17 -> 4; matrix products, arithmetic and copies ran while one was open for 22% -> 18% of each run, Pallas kernels for 0% -> 35%
where the time goes in v2:
time: 632 us; the launch traced here: 624 us
  Pallas kernels  242 us (38%)
  waiting for transfers between devices  133 us (21%)
  local copies, waits for them, and re-layouts  85.2 us (13%)
  matrix products  83.3 us (13%)
  other arithmetic  30.3 us (5%)
  blocking collectives  18.5 us (3%)
  between operations  15.7 us (2%)
  starting transfers between devices  15.4 us (2%)
    pallas_call x4, Pallas kernels, reduce_rows(): pl.pallas_call(functools.partial(reduce_kernel, n_dp, n_seq, tuple((g.sha...  133 us
    pallas_call x1, Pallas kernels, fetch(): pl.pallas_call(functools.partial(fetch_kernel, n_dp, n_seq, unit), out_sh...  109 us
    all_to_all x2, waiting for transfers between devices, exchange_sum(): got = lax.all_to_all(slabs, 'seq', split_axis=0, concat_axis=0, tiled=True)  80.6 us
    dot_general x12, matrix products, dot(): lax.dot_general(a, b, (contract, ((), ())), preferred_element_type=jnp.fl...  78.1 us
    all_gather x4, waiting for transfers between devices, gather_seq(): return lax.all_gather(shard, 'seq', axis=0, tiled=False)  37.2 us
    convert_element_type x3, local copies, waits for them, and re-layouts, local(): up_full = gather_seq(up_sum).reshape(n_seq, own, n_dp, unit).transpose(1,...  26.8 us
    convert_element_type x3, local copies, waits for them, and re-layouts, local(): qkv_full = gather_seq(qkv_sum).reshape(n_seq, own, 3, heads * HD).transpo...  20 us
    unnamed x120, local copies, waits for them, and re-layouts  19.6 us
  transfers between devices with their start and end apart: 9, of which 4 were waited for; matrix products, arithmetic and copies ran while one was open for 18% of the time, Pallas kernels for 35%

profile of v2, /device:TPU:0, one launch (start us, length us, event | category | flops | bytes accessed | tf_op | source)
XLA Modules:
  0.0 623.7 jit_solution(15173700566321967074)
XLA Ops:
  7.2 5.2 all-to-all-start
  12.4 15.3 %all-to-all-done = bf16[8,32,2048]{2,1,0:T(8,128)(2,1)S(1)} async-done(((bf16[8,32,2048]{2,1,0:T(8,128)(2,1)}), bf16[8,32,2048]{2,1,0:T(8,128)(2,1)S(1)}, u32[]{:S(2)}, u32[]{:S(2)}) %all-to-all-start) | async-done | bytes 1048608 | tf_op jit(solution)/shard_map/all_to_all | solution.py:525
  34.6 108.9 %fetch.1 = (bf16[4,128,2048]{2,1,0:T(8,128)(2,1)}, bf16[4,128,2048]{2,1,0:T(8,128)(2,1)}, f32[8,32,128]{2,1,0:T(8,128)}, bf16[8,256,2048]{2,1,0:T(8,128)(2,1)}, bf16[8,256,2048]{2,1,0:T(8,128)(2,1)}) custom-call(bf16[128,2048]{1,0:T(8,128)(2,1)} %bitcast.159, bf16[128,2048]{1,0:T(8,128)(2,1)} %bitcast.164, f32[32,128]{1,0:T(8,128)} %pad_bitcast_fusion.refs_2_, ...), custom_call_target="tpu_custom_call" | custom-call | bytes 200000000 | tf_op jit(solution)/shard_map/fetch/pallas_call | solution.py:276
  150.9 6.4 %multiply_convert_fusion = (bf16[512,2048]{1,0:T(8,128)(2,1)}, f32[512,2048]{1,0:T(8,128)S(1)}) fusion(f32[2048]{0:T(1024)S(1)} %bitcast.205, bf16[512,2048]{1,0:T(8,128)(2,1)S(1)} %bitcast.176, bf16[2048,2048]{1,0:T(8,128)(2,1)S(1)} %bitcast.212), kind=kOutput, calls=%fused_computation.21 | convolution fusion | flops 4301258752 | bytes 16785408 | tf_op jit(solution)/shard_map/dot_general | solution.py:448
  157.3 7.2 %fusion.45 = (f32[2048]{0:T(1024)S(1)}, bf16[512,2048]{1,0:T(8,128)(2,1)}) fusion(f32[512,2048]{1,0:T(8,128)S(1)} %get-tuple-element.106, f32[2048]{0:T(1024)S(1)} %bitcast.206, bf16[512,2048]{1,0:T(8,128)(2,1)S(1)} %bitcast.213, bf16[2048,2048]{1,0:T(8,128)(2,1)S(1)} %bitcast.210), kind=kOutput, calls=%fused_computation.143 | convolution fusion | flops 4307548160 | bytes 16793600 | tf_op jit(solution)/shard_map/dot_general | solution.py:448
  174.7 7.9 %convolution_add_fusion = f32[512,1536]{1,0:T(8,128)} fusion(bf16[512,2048]{1,0:T(8,128)(2,1)S(1)} %copy-done.12, bf16[2048,1536]{1,0:T(8,128)(2,1)} %all-gather.12.cloned.1.call-done, f32[1536]{0:T(1024)S(1)} %add.161), kind=kOutput, calls=%fused_computation.27 | convolution fusion | flops 3222011904 | bytes 11540480 | tf_op jit(solution)/shard_map/dot_general | solution.py:448
  182.6 4.2 reshape.427
  201.1 6.1 fusion.47
  207.2 11.4 %fusion.40 = (f32[2048]{0:T(1024)S(1)}, f32[2048]{0:T(1024)S(1)}, bf16[512,2048]{1,0:T(8,128)(2,1)}, f32[2048]{0:T(1024)S(1)}, f32[2048]{0:T(1024)S(1)}, /*index=5*/bf16[512,2048]{1,0:T(8,128)(2,1)}) fusion(f32[512]{0:T(512)S(1)} %get-tuple-element.99, f32[512]{0:T(512)S(1)} %get-tuple-element.97, bf16[4,128,2048]{2,1,0:T(8,128)(2,1)S(1)} %copy-done.1, ...), kind=kOutput, calls=%fused_computation.138 | convolution fusion | flops 4311736320 | bytes 21032960 | tf_op jit(solution)/shard_map/dot_general | solution.py:448
  222.2 21.1 %reduce_3.1 = (bf16[64,2048]{1,0:T(8,128)(2,1)}, f32[16,256]{1,0:T(8,128)}) custom-call(bf16[512,2048]{1,0:T(8,128)(2,1)} %bitcast.160, f32[128,256]{1,0:T(8,128)} %reshape.445.refs_1_), custom_call_target="tpu_custom_call" | custom-call | bytes 100000000 | tf_op jit(solution)/shard_map/reduce_3/pallas_call | solution.py:433
  245.8 8.4 %convolution_convert_fusion.refs_0_ = bf16[2048,2048]{1,0:T(8,128)(2,1)} fusion(bf16[512,2048]{1,0:T(8,128)(2,1)} %get-tuple-element.105, bf16[512,2048]{1,0:T(8,128)(2,1)S(1)} %bitcast.216), kind=kOutput, calls=%fused_computation.1 | convolution fusion | flops 4299161600 | bytes 12582912 | tf_op jit(solution)/shard_map/dot_general | solution.py:448
  254.2 40.2 %reduce_1.1 = bf16[256,2048]{1,0:T(8,128)(2,1)} custom-call(bf16[2048,2048]{1,0:T(8,128)(2,1)} %convolution_convert_fusion.refs_0_), custom_call_target="tpu_custom_call" | custom-call | bytes 100000000 | tf_op jit(solution)/shard_map/reduce_1/pallas_call | solution.py:433
  294.5 6.8 %convolution_convert_fusion.2.refs_0_ = bf16[2048,1536]{1,0:T(8,128)(2,1)} fusion(bf16[512,2048]{1,0:T(8,128)(2,1)S(1)} %bitcast.175, bf16[512,1536]{0,1:T(8,128)(2,1)} %bitcast.178), kind=kOutput, calls=%fused_computation.3 | convolution fusion | flops 3224371200 | bytes 9961472 | tf_op jit(solution)/shard_map/dot_general | solution.py:448
  301.3 32.3 %reduce_4.1 = bf16[256,1536]{1,0:T(8,128)(2,1)} custom-call(bf16[2048,1536]{1,0:T(8,128)(2,1)} %convolution_convert_fusion.2.refs_0_), custom_call_target="tpu_custom_call" | custom-call | bytes 100000000 | tf_op jit(solution)/shard_map/reduce_4/pallas_call | solution.py:433
  335.0 18.5 %all_to_all.20 = bf16[8,32,2048]{2,1,0:T(8,128)(2,1)} all-to-all(bf16[8,32,2048]{2,1,0:T(8,128)(2,1)S(1)} %bitcast.168), channel_id=1, replica_groups=mesh['dp'=8,'seq'=4] {'dp'}, dimensions={0} | all-to-all | bytes 2097152 | tf_op jit(solution)/shard_map/all_to_all | solution.py:687
  353.4 5.3 all-to-all-start.2
  359.0 10.2 %convolution_convert_fusion.1.refs_0_ = bf16[2048,2048]{1,0:T(8,128)(2,1)} fusion(bf16[512,2048]{1,0:T(8,128)(2,1)} %get-tuple-element.67, bf16[512,2048]{1,0:T(8,128)(2,1)} %get-tuple-element.108), kind=kOutput, calls=%fused_computation.2 | convolution fusion | flops 4299161600 | bytes 12582912 | tf_op jit(solution)/shard_map/dot_general | solution.py:448
  369.2 39.7 %reduce_2.1 = bf16[256,2048]{1,0:T(8,128)(2,1)} custom-call(bf16[2048,2048]{1,0:T(8,128)(2,1)} %convolution_convert_fusion.1.refs_0_), custom_call_target="tpu_custom_call" | custom-call | bytes 100000000 | tf_op jit(solution)/shard_map/reduce_2/pallas_call | solution.py:433
  408.9 7.7 %fusion.46 = f32[512,2048]{1,0:T(8,128)S(1)} fusion(bf16[512,2048]{1,0:T(8,128)(2,1)} %get-tuple-element.105, bf16[2048,2048]{1,0:T(8,128)(2,1)} %bitcast.207), kind=kOutput, calls=%fused_computation.144 | convolution fusion | flops 4294967296 | bytes 14680064 | tf_op jit(solution)/shard_map/dot_general | solution.py:448
  419.2 31.8 %all-to-all-done.2 = bf16[4,128,2048]{2,1,0:T(8,128)(2,1)S(1)} async-done(((bf16[4,128,2048]{2,1,0:T(8,128)(2,1)}), bf16[4,128,2048]{2,1,0:T(8,128)(2,1)S(1)}, u32[]{:S(2)}, u32[]{:S(2)}) %all-to-all-start.2) | async-done | bytes 2097184 | tf_op jit(solution)/shard_map/all_to_all | solution.py:488
  451.1 4.4 all-to-all-start.1
  456.1 6.7 %convert_element_type.333 = f32[1024,2048]{1,0:T(8,128)} convert(bf16[1024,2048]{1,0:T(8,128)(2,1)} %all-gather.22.cloned.1.call-done) | non-fusion elementwise | flops 2097152 | bytes 12582912 | tf_op jit(solution)/shard_map/convert_element_type | solution.py:664
  468.1 48.7 %all-to-all-done.1 = bf16[4,128,2048]{2,1,0:T(8,128)(2,1)} async-done(((bf16[4,128,2048]{2,1,0:T(8,128)(2,1)}), bf16[4,128,2048]{2,1,0:T(8,128)(2,1)}, u32[]{:S(2)}, u32[]{:S(2)}) %all-to-all-start.1) | async-done | bytes 2097184 | tf_op jit(solution)/shard_map/all_to_all | solution.py:488
  520.7 5.4 copy.105
  526.1 8.1 %reshape.454 = f32[4,256,3,512]{1,0,3,2:T(4,128)} reshape(f32[1024,1536]{0,1:T(8,128)} %copy.105) | data formatting | bytes 12582912 | tf_op jit(solution)/shard_map/convert_element_type | solution.py:707
  534.2 6.5 %copy.106 = f32[256,3,4,512]{0,3,2,1:T(8,128)} copy(f32[256,3,4,512]{0,2,3,1:T(4,128)} %bitcast.157) | data formatting | bytes 12582912 | tf_op jit(solution)/shard_map/convert_element_type | solution.py:707
  540.7 6.8 %copy.108 = f32[256,6144]{1,0:T(8,128)} copy(f32[256,6144]{0,1:T(8,128)} %bitcast.158) | data formatting | bytes 12582912
  547.6 37.1 %all-gather.20.cloned.1.call-done = bf16[1024,2048]{1,0:T(8,128)(2,1)} async-done(((bf16[256,2048]{1,0:T(8,128)(2,1)}), bf16[1024,2048]{1,0:T(8,128)(2,1)}) %all-gather.20.cloned.1.call-update) | async-done | bytes 4194320 | tf_op jit(solution)/shard_map/all_gather | solution.py:483
  584.7 4.3 copy.135
  589.0 4.0 bitcast_bitcast_fusion
  593.0 12.0 %copy.107 = f32[256,8,4,256]{3,2,1,0:T(4,128)} copy(f32[256,8,4,256]{3,1,0,2:T(8,128)} %bitcast_bitcast_fusion) | data formatting | bytes 16777216 | tf_op jit(solution)/shard_map/convert_element_type | solution.py:671
  605.1 10.7 %reshape.452 = f32[256,8192]{1,0:T(8,128)} reshape(f32[256,8,4,256]{3,2,1,0:T(4,128)} %copy.107) | data formatting | bytes 16777216 | tf_op jit(solution)/shard_map/convert_element_type | solution.py:671
  (220 shorter events, 58.4 us)
Async XLA Ops:
  7.2 20.6 %all-to-all-start = ((bf16[8,32,2048]{2,1,0:T(8,128)(2,1)}), bf16[8,32,2048]{2,1,0:T(8,128)(2,1)S(1)}, u32[]{:S(2)}, u32[]{:S(2)}) async-start(bf16[8,32,2048]{2,1,0:T(8,128)(2,1)} %bitcast.179), calls=%async_computation | async-start | bytes 2097152 | tf_op jit(solution)/shard_map/all_to_all | solution.py:525
  12.4 157.0 %all-gather.14.cloned.1.call-start = ((), (), s32[]{:S(2)}) async-start(), calls=%async_computation.5 | async-start | bytes 2359296 | tf_op jit(solution)/shard_map/all_gather | solution.py:530
  28.5 146.2 %all-gather.12.cloned.1.call-start = ((), (), s32[]{:S(2)}) async-start(), calls=%async_computation.4 | async-start | bytes 7077888 | tf_op jit(solution)/shard_map/all_gather | solution.py:479
  31.5 2.5 copy-start.31
  31.5 2.5 copy-start.32
  33.8 299.9 %all-gather.16.cloned.1.call-start = ((), (), s32[]{:S(2)}) async-start(), calls=%async_computation.6 | async-start | bytes 1638400 | tf_op jit(solution)/shard_map/all_gather | solution.py:483
  34.6 110.2 %copy-start.7 = (bf16[1,128,2048]{2,1,0:T(8,128)(2,1)S(1)}, bf16[1,128,2048]{2,1,0:T(8,128)(2,1)}, u32[]{:S(2)}) copy-start(bf16[1,128,2048]{2,1,0:T(8,128)(2,1)} %param.15) | copy-start | bytes 1572868
  143.5 3.4 copy-start
  146.9 4.0 copy-start.39
  147.6 9.7 %slice-start = ((s8[8388608]{0:T(1024)(128)(4,1)}), s8[4194304]{0:T(1024)(128)(4,1)S(1)}, s32[]{:S(2)}) async-start(s8[8388608]{0:T(1024)(128)(4,1)} %bitcast.208), calls=%async_computation.10 | async-start | bytes 8388608
  150.9 6.4 %slice-start.1 = ((s8[8388608]{0:T(1024)(128)(4,1)}), s8[4194304]{0:T(1024)(128)(4,1)S(1)}, s32[]{:S(2)}) async-start(s8[8388608]{0:T(1024)(128)(4,1)} %bitcast.208), calls=%async_computation.11 | async-start | bytes 8388608
  150.9 6.4 %copy-start.40 = (bf16[4,128,2048]{2,1,0:T(8,128)(2,1)S(1)}, bf16[4,128,2048]{2,1,0:T(8,128)(2,1)}, u32[]{:S(2)}) copy-start(bf16[4,128,2048]{2,1,0:T(8,128)(2,1)} %get-tuple-element.25) | copy-start | bytes 6291460
  169.4 3.3 copy-start.41
  190.1 2.9 copy-start.9
  200.9 6.2 %copy-start.18 = (bf16[512,3,2,256]{0,3,2,1:T(8,128)(2,1)}, bf16[512,3,2,256]{0,3,2,1:T(8,128)(2,1)S(1)}, u32[]{:S(2)}) copy-start(bf16[512,3,2,256]{0,3,2,1:T(8,128)(2,1)S(1)} %copy.103) | copy-start | bytes 4718596
  201.1 6.1 copy-start.1
  201.1 6.1 copy-start.43
  207.2 12.3 %copy-start.11 = (bf16[2,256,512]{2,1,0:T(8,128)(2,1)S(1)}, bf16[2,256,512]{2,1,0:T(8,128)(2,1)}, u32[]{:S(2)}) copy-start(bf16[2,256,512]{2,1,0:T(8,128)(2,1)} %get-tuple-element.104) | copy-start | bytes 1572868
  207.2 12.3 %copy-start.42 = (bf16[4,128,2048]{2,1,0:T(8,128)(2,1)S(1)}, bf16[4,128,2048]{2,1,0:T(8,128)(2,1)}, u32[]{:S(2)}) copy-start(bf16[4,128,2048]{2,1,0:T(8,128)(2,1)} %get-tuple-element.25) | copy-start | bytes 6291460
  245.8 210.3 %all-gather.22.cloned.1.call-start = ((), (), s32[]{:S(2)}) async-start(), calls=%async_computation.9 | async-start | bytes 5242880 | tf_op jit(solution)/shard_map/all_gather | solution.py:483
  254.2 40.3 %copy-start.17 = (bf16[4,128,2048]{2,1,0:T(8,128)(2,1)S(1)}, bf16[4,128,2048]{2,1,0:T(8,128)(2,1)}, u32[]{:S(2)}) copy-start(bf16[4,128,2048]{2,1,0:T(8,128)(2,1)} %get-tuple-element.68) | copy-start | bytes 6291460
  294.5 226.3 %all-gather.18.cloned.1.call-start = ((), (), s32[]{:S(2)}) async-start(), calls=%async_computation.7 | async-start | bytes 3932160 | tf_op jit(solution)/shard_map/all_gather | solution.py:483
  353.4 97.6 %all-to-all-start.2 = ((bf16[4,128,2048]{2,1,0:T(8,128)(2,1)}), bf16[4,128,2048]{2,1,0:T(8,128)(2,1)S(1)}, u32[]{:S(2)}, u32[]{:S(2)}) async-start(bf16[4,128,2048]{2,1,0:T(8,128)(2,1)} %bitcast.173), calls=%async_computation.2 | async-start | bytes 4194304 | tf_op jit(solution)/shard_map/all_to_all | solution.py:488
  358.8 225.9 %all-gather.20.cloned.1.call-start = ((), (), s32[]{:S(2)}) async-start(), calls=%async_computation.8 | async-start | bytes 5242880 | tf_op jit(solution)/shard_map/all_gather | solution.py:483
  408.9 7.7 %copy-start.6 = (bf16[2,8,32,2048]{3,2,1,0:T(8,128)(2,1)S(1)}, bf16[2,8,32,2048]{3,2,1,0:T(8,128)(2,1)}, u32[]{:S(2)}) copy-start(bf16[2,8,32,2048]{3,2,1,0:T(8,128)(2,1)} %copy-done.5) | copy-start | bytes 6291460
  419.2 36.3 %copy-start.2 = (bf16[1,128,2048]{2,1,0:T(8,128)(2,1)S(1)}, bf16[1,128,2048]{2,1,0:T(8,128)(2,1)}, u32[]{:S(2)}) copy-start(bf16[1,128,2048]{2,1,0:T(8,128)(2,1)} %param.14) | copy-start | bytes 1572868
  451.1 11.7 %copy-start.3 = (bf16[4,128,2048]{2,1,0:T(8,128)(2,1)}, bf16[4,128,2048]{2,1,0:T(8,128)(2,1)S(1)}, u32[]{:S(2)}) copy-start(bf16[4,128,2048]{2,1,0:T(8,128)(2,1)S(1)} %all-to-all-done.2) | copy-start | bytes 6291460
  451.1 65.7 %all-to-all-start.1 = ((bf16[4,128,2048]{2,1,0:T(8,128)(2,1)}), bf16[4,128,2048]{2,1,0:T(8,128)(2,1)}, u32[]{:S(2)}, u32[]{:S(2)}) async-start(bf16[4,128,2048]{2,1,0:T(8,128)(2,1)} %bitcast.19), calls=%async_computation.1 | async-start | bytes 4194304 | tf_op jit(solution)/shard_map/all_to_all | solution.py:488
  456.1 9.5 %copy-start.10 = (bf16[8,32,2048]{2,1,0:T(8,128)(2,1)S(1)}, bf16[8,32,2048]{2,1,0:T(8,128)(2,1)}, u32[]{:S(2)}) copy-start(bf16[8,32,2048]{2,1,0:T(8,128)(2,1)} %all_to_all.20) | copy-start | bytes 3145732
  463.8 3.4 copy-start.4
  465.5 150.3 %copy-start.30 = (f32[256]{0:T(256)}, f32[256]{0:T(256)S(1)}, u32[]{:S(2)}) copy-start(f32[256]{0:T(256)S(1)} %get-tuple-element.140) | copy-start | bytes 3076
  467.7 51.2 %copy-start.8 = (bf16[1,128,2048]{2,1,0:T(8,128)(2,1)S(1)}, bf16[1,128,2048]{2,1,0:T(8,128)(2,1)}, u32[]{:S(2)}) copy-start(bf16[1,128,2048]{2,1,0:T(8,128)(2,1)} %param.15) | copy-start | bytes 1572868
  (23 other events, 42.8 us)
Sparse Core Ops, SparseCore 0:
  28.6 35.8 all-gather.13
  66.9 70.8 all-gather.11
  245.9 32.3 all-gather.15
  294.6 100.4 all-gather.21
  396.5 108.2 all-gather.17
  506.2 78.4 all-gather.19
